TPU v7x, 256 devices: a whole 4x4x8 slice. The times are simulated.
256 devices in a mesh: ctx: 128 (over x, y_hi, z, core), head: 2 (over y_lo).
Axes of the slice: x: 4, y: 4 (y_hi: 2, y_lo: 2; y = y_hi * 2 + y_lo), z: 8, core: 2. Of those that a mesh axis runs over, the one named last changes fastest.
Arguments:
- queries: bfloat16 [16384, 2048], P('ctx', 'head'), may hold values from -160 to 160
- rotated_keys: bfloat16 [16384, 512], P('ctx', 'head'), may hold values from -6 to 6
- value_matrix: bfloat16 [16384, 512], P('ctx', 'head'), may hold values from -6 to 6
- doc_lengths: int32 [8], replicated, may hold values from 1 to 12288, 16384 in all
- scored: int32 [512], P('ctx'), may hold values from 0 to 127, as said below
- residual: bfloat16 [512, 4096], P('ctx', 'head'), may hold values from -18 to 18
- norm_gain: float32 [4096], P('head'), may hold values from 0.5 to 1.5
- out_weight: bfloat16 [2048, 4096], P('head'), may hold values from -0.5 to 0.5
- lm_weight: bfloat16 [4096, 128256], P('head', 'ctx'), may hold values from -0.40625 to 0.40625
- token_ids: int32 [512], replicated, may hold values from 0 to 128255
- old_logp: float32 [512], replicated, may hold values from -24 to -9
- advantage: float32 [512], replicated, may hold values from -3 to 3
Outputs:
- attended: bfloat16 [16384, 2048], P('ctx', 'head')
- log_probs: float32 [512], replicated
- token_loss: float32 [512], replicated
Inputs may be any that keep to these rules, and one draw needn't show every extreme that they name: `scored`: each aligned block of 4 entries holds distinct increasing offsets. `doc_lengths`: the longest document has exactly three quarters of 16384 positions.
All inputs are finite; a program needn't handle non-finite values.
Results may differ from a plain program's by a relative error of at most 0.0065.
Values may be sent and summed in bfloat16 or wider, within the bound.
A program may use at most 128 MiB of HBM per device.

v0:
```python
import math

import jax
import jax.numpy as jnp
from jax import lax
from jax.sharding import Mesh
from jax.sharding import PartitionSpec as P

HEAD_SIZE = 128
CTX = ("ctx_0", "ctx_1", "ctx_2", "ctx_3")
CTX_HEAD = ("ctx_0", "ctx_1", "ctx_2", "ctx_3", "head")


masked_score = -1e30


def side_by_side(arrays, axis, dim, along):
    both = jnp.concatenate(arrays, axis=along)
    whole, at, outs = (lax.all_gather(both, axis, axis=dim, tiled=True), 0, [])
    for a in arrays:
        outs.append(lax.slice_in_dim(whole, at, at + a.shape[along], axis=along))
        at += a.shape[along]
    return tuple(outs)


def in_blocks(shard, dim, peers):
    before, after = (shard.shape[:dim], shard.shape[dim + 1 :])
    return jnp.moveaxis(shard.reshape(*before, peers, -1, *after), dim, 0)


def sum_at_owner(shard, axis, dim):
    pieces = in_blocks(shard, dim, lax.axis_size(axis))
    arrived = lax.all_to_all(pieces, axis, split_axis=0, concat_axis=0, tiled=True)
    return arrived.astype(jnp.float32).sum(axis=0)


def sent_to_all(shard, axis):
    peers = lax.axis_size(axis)
    return lax.all_to_all(
        jnp.broadcast_to(shard[None], (peers, *shard.shape)), axis, 0, 0, tiled=True
    )


def of_everyone(shard, axis):
    everything = sent_to_all(shard, axis)
    return jnp.sum(everything, axis=0)


def all_in_one(shard, axis):
    leaves = jax.tree.leaves(shard)
    order = sorted(range(len(leaves)), key=lambda k: -leaves[k].size)
    width = (1, *leaves[order[0]].shape)[-1]
    lines = [
        jnp.pad(leaves[k].reshape(-1), (0, -leaves[k].size % width)).reshape(-1, width)
        for k in order
    ]
    both, at, found = (lax.all_gather(jnp.concatenate(lines), axis), 0, {})
    for k, line in zip(order, lines):
        slab = both[:, at : at + len(line)].reshape(len(both), -1)
        found[k] = slab[:, : leaves[k].size].reshape(-1, *leaves[k].shape)
        at += len(line)
    numbers = iter(range(len(leaves)))
    return jax.tree.map(lambda _: found[next(numbers)], shard)


def merged_by_axis(shard, axes, combine):
    for axis in axes:
        pieces = all_in_one(shard, axis)
        shard = jax.tree.map(lambda part: part[0], pieces)
        for k in range(1, lax.axis_size(axis)):
            shard = combine(shard, jax.tree.map(lambda part: part[k], pieces))
    return shard


def doc_index(positions, doc_ends):
    return jnp.sum((positions[:, None] >= doc_ends[None, :]).astype(jnp.int32), axis=1)


def attend_rows(running, context, key_part, value_part, offset):
    query_heads, query_pos, query_doc, doc_ends, first_start, skipping = context
    row_top, row_total, accumulated = running
    row_count = key_part.shape[0]
    kv_heads = query_heads.shape[1]
    key_head_rows = key_part.reshape(row_count, kv_heads, HEAD_SIZE)
    value_head_rows = value_part.reshape(row_count, kv_heads, HEAD_SIZE)
    scores = jnp.einsum(
        "qkgd,rkd->kgqr", query_heads, key_head_rows, preferred_element_type=jnp.float32
    ) * HEAD_SIZE ** (-0.5)
    key_pos = offset + jnp.arange(row_count, dtype=jnp.int32)
    allowed = (
        (key_pos[None, :] <= query_pos[:, None])
        & (key_pos[None, :] >= 0)
        & (doc_index(key_pos, doc_ends)[None, :] == query_doc[:, None])
    )
    scores = jnp.where(allowed, scores, masked_score)
    new_top = jnp.maximum(row_top, jnp.max(scores, axis=-1))
    weights = jnp.where(allowed, jnp.exp(scores - new_top[..., None]), 0.0)
    rescale = jnp.exp(row_top - new_top)
    row_total = row_total * rescale + jnp.sum(weights, axis=-1)
    update = jnp.einsum(
        "kgqr,rkd->kgqd",
        weights.astype(jnp.bfloat16),
        value_head_rows,
        preferred_element_type=jnp.float32,
    )
    accumulated = accumulated * rescale[..., None] + update
    return (new_top, row_total, accumulated)


def attend_piece(running, shard_piece, context):
    key_rows, value_rows = shard_piece
    row_count = key_rows.shape[0]
    block_rows = math.gcd(row_count, 512)
    block_count = row_count // block_rows

    def one_block(block_index, carried):
        start_row = block_index * block_rows
        key_part = lax.dynamic_slice_in_dim(key_rows, start_row, block_rows, 0)
        value_part = lax.dynamic_slice_in_dim(value_rows, start_row, block_rows, 0)
        return attend_rows(carried, context, key_part, value_part, start_row)

    return lax.fori_loop(0, block_count, one_block, running)


def combine(earlier, later):
    top_one, sum_one, target_one = earlier
    top_two, sum_two, target_two = later
    new_top = jnp.maximum(top_one, top_two)
    merged_sum = sum_one * jnp.exp(top_one - new_top) + sum_two * jnp.exp(top_two - new_top)
    return (new_top, merged_sum, target_one + target_two)


def per_device(
    queries,
    rotated_keys,
    value_matrix,
    doc_lengths,
    scored,
    residual,
    norm_gain,
    out_weight,
    lm_weight,
    token_ids,
    old_logp,
    advantage,
):
    tok_rows = queries.shape[0]
    kv_heads = rotated_keys.shape[1] // HEAD_SIZE
    group_count = queries.shape[1] // rotated_keys.shape[1]
    my_index = lax.axis_index(CTX)
    doc_ends = jnp.cumsum(doc_lengths)
    doc_starts = doc_ends - doc_lengths
    query_pos = my_index * tok_rows + jnp.arange(tok_rows, dtype=jnp.int32)
    query_doc = doc_index(query_pos, doc_ends)
    first_start = jnp.max(jnp.where(doc_starts <= query_pos[0], doc_starts, 0))
    query_heads = queries.reshape(tok_rows, kv_heads, group_count, HEAD_SIZE)
    context = (query_heads, query_pos, query_doc, doc_ends, first_start, False)
    state_shape = (kv_heads, group_count, tok_rows)
    initial = (
        jnp.full(state_shape, masked_score, jnp.float32),
        jnp.zeros(state_shape, jnp.float32),
        jnp.zeros(state_shape + (HEAD_SIZE,), jnp.float32),
    )
    row_top, row_total, accumulated = attend_piece(
        initial, side_by_side((rotated_keys, value_matrix), CTX, 0, 1), context
    )
    result = accumulated / row_total[..., None]
    attended = (
        jnp.transpose(result, (2, 0, 1, 3))
        .reshape(tok_rows, kv_heads * group_count * HEAD_SIZE)
        .astype(jnp.bfloat16)
    )
    chosen = jnp.take(attended, scored, axis=0)
    partial_value = jnp.dot(chosen, out_weight, preferred_element_type=jnp.float32)
    projected = sum_at_owner(partial_value.astype(jnp.bfloat16), "head", 1)
    hidden = residual.astype(jnp.float32) + projected
    squares = of_everyone(jnp.sum(hidden * hidden, axis=1), "head")
    full_width = hidden.shape[1] * lax.axis_size("head")
    normed = (
        hidden * lax.rsqrt(squares[:, None] / full_width + 1e-05) * norm_gain[None, :]
    ).astype(jnp.bfloat16)
    partial_logits = jnp.dot(
        lax.all_gather(normed, CTX, axis=0, tiled=True),
        lm_weight,
        preferred_element_type=jnp.float32,
    )
    logits = sum_at_owner(partial_logits.astype(jnp.bfloat16), "head", 1)
    vocab_rows = logits.shape[1]
    vocab_start = (
        my_index * vocab_rows * lax.axis_size("head") + lax.axis_index("head") * vocab_rows
    )
    local_ids = token_ids - vocab_start
    matches = local_ids[:, None] == jnp.arange(vocab_rows, dtype=jnp.int32)[None, :]
    target_part = jnp.sum(jnp.where(matches, logits, 0.0), axis=1)
    local_top = jnp.max(logits, axis=1)
    sum_part = jnp.sum(jnp.exp(logits - local_top[:, None]), axis=1)
    global_top, exp_total, target = merged_by_axis(
        (local_top, sum_part, target_part), CTX_HEAD, combine
    )
    log_probs = target - global_top - jnp.log(exp_total)
    ratio = jnp.exp(jnp.clip(log_probs - old_logp, -4.0, 4.0))
    token_loss = -jnp.minimum(ratio * advantage, jnp.clip(ratio, 0.8, 1.2) * advantage)
    return (attended, log_probs, token_loss)


def solution(mesh):
    finer = Mesh(
        mesh.devices.reshape(4, 2, 8, 2, mesh.shape["head"]),
        ("ctx_0", "ctx_1", "ctx_2", "ctx_3", "head"),
    )
    placed = (
        P(CTX, "head"),
        P(CTX, "head"),
        P(CTX, "head"),
        P(),
        P(CTX),
        P(CTX, "head"),
        P("head"),
        P("head", None),
        P("head", CTX),
        P(),
        P(),
        P(),
    )
    return jax.shard_map(
        per_device,
        mesh=finer,
        in_specs=placed,
        out_specs=(P(CTX, "head"), P(), P()),
        check_vma=False,
    )
```

profile of v0, /device:TPU:8, one launch (start us, length us, event | category | flops | bytes accessed | tf_op | source)
XLA Modules:
  0.0 490.7 jit_solution(17511669347726125021)
XLA Ops:
  10.7 1.1 copy.48
  13.5 136.4 %all-gather.14.cloned.1.call-done = bf16[16384,512]{0,1:T(8,128)(2,1)} async-done(((bf16[128,512]{0,1:T(8,128)(2,1)}), bf16[16384,512]{0,1:T(8,128)(2,1)}) %all-gather.14.cloned.1.call-update) | async-done | bytes 16777232 | tf_op jit(solution)/shard_map/all_gather | solution.py:19
  149.9 11.4 %fusion.76 = (bf16[16384,256]{0,1:T(8,128)(2,1)}, bf16[16384,256]{0,1:T(8,128)(2,1)}) fusion(bf16[16384,512]{0,1:T(8,128)(2,1)} %all-gather.14.cloned.1.call-done), kind=kLoop, calls=%fused_computation.157 | loop fusion | bytes 33554432 | tf_op jit(solution)/shard_map/slice | solution.py:21
  161.3 113.7 %while.18 = (s32[]{:T(128)}, f32[2,4,128]{2,1,0:T(4,128)S(1)}, f32[2,4,128]{2,1,0:T(4,128)S(1)}, f32[2,4,128,128]{3,2,1,0:T(8,128)S(1)}, s32[8]{0:T(128)S(1)}, /...) while((s32[]{:T(128)}, f32[2,4,128]{2,1,0:T(4,128)S(1)}, ...), condition=%wide.region_6.7_spmd.clone, body=%wide.region_2.6_spmd.clone.sunk | while | flops 275925120 | bytes 9515759 | solution.py:122
  161.7 1.1 constant_dynamic-slice_fusion.3
  165.3 1.1 constant_dynamic-slice_fusion.3
  168.8 1.1 constant_dynamic-slice_fusion.3
  172.4 1.1 constant_dynamic-slice_fusion.3
  175.9 1.1 constant_dynamic-slice_fusion.3
  179.5 1.1 constant_dynamic-slice_fusion.3
  276.3 4.6 convolution_convert_fusion
  280.9 5.0 %all_to_all.16 = bf16[2,4,2048]{2,1,0:T(4,128)(2,1)S(1)} all-to-all(bf16[2,4,2048]{2,1,0:T(4,128)(2,1)S(1)} %bitcast.366), channel_id=1, replica_groups=mesh['ctx_0'=4,'ctx_1'=2,'ctx_2'=8,'ctx_3'=2,'head'=2] {'head'}, dimensions={0} | all-to-all | bytes 65536 | tf_op jit(solution)/shard_map/all_to_all | solution.py:33
  286.1 6.1 %all_to_all.17 = f32[2,1,4]{2,1,0:T(1,128)S(1)} all-to-all(f32[2,1,4]{2,1,0:T(1,128)S(1)} %broadcast_in_dim.94), channel_id=1, replica_groups=mesh['ctx_0'=4,'ctx_1'=2,'ctx_2'=8,'ctx_3'=2,'head'=2] {'head'}, dimensions={0} | all-to-all | bytes 64 | tf_op jit(solution)/shard_map/all_to_all | solution.py:39
  292.9 114.9 %all-gather.16.cloned.1.call-done = bf16[128,4,2048]{2,1,0:T(4,128)(2,1)} async-done(((bf16[1,4,2048]{2,1,0:T(4,128)(2,1)}), bf16[128,4,2048]{2,1,0:T(4,128)(2,1)}) %all-gather.16.cloned.1.call-update) | async-done | bytes 2097168 | tf_op jit(solution)/shard_map/all_gather | solution.py:183
  407.8 2.5 reshape.1099
  410.4 4.5 convolution_convert_fusion.1
  414.9 1.2 reshape.1077
  416.1 5.0 %all-to-all-start.2 = ((bf16[2,512,501]{1,2,0:T(8,128)(2,1)}), bf16[2,512,501]{1,2,0:T(8,128)(2,1)S(1)}, u32[]{:S(2)}, u32[]{:S(2)}) async-start(bf16[2,512,501]{1,2,0:T(8,128)(2,1)} %bitcast.8), calls=%async_computation.2 | async-start | bytes 2064384 | tf_op jit(solution)/shard_map/all_to_all | solution.py:33
  421.1 12.3 %all-to-all-done.2 = bf16[2,512,501]{1,2,0:T(8,128)(2,1)S(1)} async-done(((bf16[2,512,501]{1,2,0:T(8,128)(2,1)}), bf16[2,512,501]{1,2,0:T(8,128)(2,1)S(1)}, u32[]{:S(2)}, u32[]{:S(2)}) %all-to-all-start.2) | async-done | bytes 1026080 | tf_op jit(solution)/shard_map/all_to_all | solution.py:33
  434.0 12.2 %all-gather.6 = f32[4,3,512]{2,1,0:T(4,128)S(1)} all-gather(f32[1,3,512]{2,1,0:T(4,128)S(1)} %maximum_bitcast_fusion), channel_id=2, replica_groups=mesh['ctx_0'=4,'ctx_1'=2,'ctx_2'=8,'ctx_3'=2,'head'=2] {'ctx_0'}, dimensions={0}, use_global_device_ids=true | all-gather | bytes 30720 | tf_op jit(solution)/shard_map/all_gather | solution.py:57
  446.3 5.9 %all-gather.7 = f32[2,3,512]{2,1,0:T(4,128)S(1)} all-gather(f32[1,3,512]{2,1,0:T(4,128)S(1)} %maximum_bitcast_fusion.1), channel_id=3, replica_groups=mesh['ctx_0'=4,'ctx_1'=2,'ctx_2'=8,'ctx_3'=2,'head'=2] {'ctx_1'}, dimensions={0}, use_global_device_ids=true | all-gather | bytes 18432 | tf_op jit(solution)/shard_map/all_gather | solution.py:57
  452.2 24.6 %all-gather.8 = f32[8,3,512]{2,1,0:T(4,128)S(1)} all-gather(f32[1,3,512]{2,1,0:T(4,128)S(1)} %maximum_bitcast_fusion.2), channel_id=4, replica_groups=mesh['ctx_0'=4,'ctx_1'=2,'ctx_2'=8,'ctx_3'=2,'head'=2] {'ctx_2'}, dimensions={0}, use_global_device_ids=true | all-gather | bytes 55296 | tf_op jit(solution)/shard_map/all_gather | solution.py:57
  476.9 1.8 all-gather.9
  478.8 4.4 all-gather.10
  (436 shorter events, 113.4 us)
Async XLA Ops:
  7.2 142.7 %all-gather.14.cloned.1.call-start = ((), (), s32[]{:S(2)}) async-start(), calls=%async_computation.3 | async-start | bytes 16908288 | tf_op jit(solution)/shard_map/all_gather | solution.py:19
  9.8 398.0 %all-gather.16.cloned.1.call-start = ((), (), s32[]{:S(2)}) async-start(), calls=%async_computation.4 | async-start | bytes 2113536 | tf_op jit(solution)/shard_map/all_gather | solution.py:183
  275.6 5.2 %copy-start = (bf16[128,1024]{1,0:T(8,128)(2,1)}, bf16[128,1024]{1,0:T(8,128)(2,1)S(1)}, u32[]{:S(2)}) copy-start(bf16[128,1024]{1,0:T(8,128)(2,1)S(1)} %convert_element_type.47) | copy-start | bytes 786436
  276.2 9.7 %copy-start.1 = (bf16[4,2048]{1,0:T(4,128)(2,1)S(1)}, bf16[4,2048]{1,0:T(4,128)(2,1)}, u32[]{:S(2)}) copy-start(bf16[4,2048]{1,0:T(4,128)(2,1)} %param.19) | copy-start | bytes 49156
  276.2 16.0 %copy-start.2 = (f32[2048]{0:T(1024)S(1)}, f32[2048]{0:T(1024)}, u32[]{:S(2)}) copy-start(f32[2048]{0:T(1024)} %param.20) | copy-start | bytes 24580
  414.9 6.2 %copy-start.5 = (s32[512]{0:T(512)S(1)}, s32[512]{0:T(512)}, u32[]{:S(2)}) copy-start(s32[512]{0:T(512)} %param.23) | copy-start | bytes 6148
  416.1 17.4 %all-to-all-start.2 = ((bf16[2,512,501]{1,2,0:T(8,128)(2,1)}), bf16[2,512,501]{1,2,0:T(8,128)(2,1)S(1)}, u32[]{:S(2)}, u32[]{:S(2)}) async-start(bf16[2,512,501]{1,2,0:T(8,128)(2,1)} %bitcast.8), calls=%async_computation.2 | async-start | bytes 2064384 | tf_op jit(solution)/shard_map/all_to_all | solution.py:33
  421.1 62.1 %copy-start.3 = (f32[512]{0:T(512)S(1)}, f32[512]{0:T(512)}, u32[]{:S(2)}) copy-start(f32[512]{0:T(512)} %param.25) | copy-start | bytes 6148
  421.1 62.1 %copy-start.4 = (f32[512]{0:T(512)S(1)}, f32[512]{0:T(512)}, u32[]{:S(2)}) copy-start(f32[512]{0:T(512)} %param.24) | copy-start | bytes 6148
Sparse Core Ops, SparseCore 0:
  12.3 137.5 all-gather.13
  293.0 114.7 all-gather.15
where the time goes:
time: 493 us; the launch traced here: 491 us
  waiting for transfers between devices  264 us (54%)
  blocking collectives  60 us (12%)
  matrix products  56.6 us (11%)
  local copies, waits for them, and re-layouts  53.7 us (11%)
  other arithmetic  34.7 us (7%)
  between operations  14.3 us (3%)
  starting transfers between devices  5.08 us (1%)
    all_gather x1, waiting for transfers between devices, side_by_side(): whole, at, outs = (lax.all_gather(both, axis, axis=dim, tiled=True), 0, [])  136 us
    all_gather x1, waiting for transfers between devices, per_device(): lax.all_gather(normed, CTX, axis=0, tiled=True)  115 us
    all_gather x5, blocking collectives, all_in_one(): both, at, found = (lax.all_gather(jnp.concatenate(lines), axis), 0, {})  48.9 us
    dynamic_slice x32, local copies, waits for them, and re-layouts, one_block(): value_part = lax.dynamic_slice_in_dim(value_rows, start_row, block_rows, 0)  34.3 us
    dot_general x32, matrix products, attend_rows(): jnp.einsum('kgqr,rkd->kgqd', weights.astype(jnp.bfloat16), value_head_row...  30.3 us
    dot_general x32, matrix products, attend_rows(): jnp.einsum('qkgd,rkd->kgqr', query_heads, key_head_rows, preferred_elemen...  17.2 us
    reduce_sum x32, other arithmetic, attend_rows(): row_total = row_total * rescale + jnp.sum(weights, axis=-1)  16.7 us
    all_to_all x1, waiting for transfers between devices, sum_at_owner(): lax.all_to_all(pieces, axis, split_axis=0, concat_axis=0, tiled=True)  12.3 us
  transfers between devices with their start and end apart: 3, of which 3 were waited for; matrix products, arithmetic and copies ran while one was open for 1% of the time, Pallas kernels for 0%

commit v1 on v0

v1 whole, which is shorter than its diff:
```python
import functools
import math

import jax
import jax.numpy as jnp
from jax import lax
from jax.experimental import pallas as pl
from jax.experimental.pallas import tpu as pltpu
from jax.sharding import Mesh
from jax.sharding import PartitionSpec as P

HEAD_SIZE = 128
CTX = ("x", "yh", "z", "core")
NAMES = ("x", "yh", "z", "core", "head")
NEG = -1e30
SCALE = HEAD_SIZE**-0.5 * math.log2(math.e)
MESH = pl.DeviceIdType.MESH
VMEM = pltpu.VMEM


def remote(src, dst, send_sem, recv_sem, **where):
    return pltpu.make_async_remote_copy(
        src_ref=src,
        dst_ref=dst,
        send_sem=send_sem,
        recv_sem=recv_sem,
        device_id=where,
        device_id_type=MESH,
    )


def greet(peers):
    barrier = pltpu.get_barrier_semaphore()
    for where in peers:
        pl.semaphore_signal(barrier, inc=1, device_id=where, device_id_type=MESH)
    pl.semaphore_wait(barrier, len(peers))


def exchange_kernel(
    sizes,
    kv_ref,
    q_ref,
    kvbuf,
    qbuf,
    first_send,
    first_recv,
    up_send,
    up_recv,
    down_send,
    down_recv,
    q_send,
    q_recv,
):
    xs, zs = sizes
    x, yh, z, kc = (lax.axis_index(n) for n in CTX)
    up, down = (lax.rem(z + 1, zs), lax.rem(z + zs - 1, zs))
    shift = lax.rem(z, xs)
    tx = lax.rem(x + z, xs)
    mine = 2 * yh + kc
    peers = []
    for dx in range(xs):
        for dy in range(2):
            for dk in range(2):
                if dx or dy or dk:
                    peers.append(
                        {
                            "x": lax.rem(x + dx, xs),
                            "yh": lax.rem(yh + dy, 2),
                            "core": lax.rem(kc + dk, 2),
                        }
                    )
    peers.append({"z": up})
    peers.append({"z": down})
    greet(peers)

    def first(dy, dk):
        ty, tk = (lax.rem(yh + dy, 2), lax.rem(kc + dk, 2))
        return remote(
            kv_ref.at[tk],
            kvbuf.at[z, mine],
            first_send.at[2 * dy + dk],
            first_recv.at[mine],
            x=tx,
            yh=ty,
            core=tk,
        )

    def first_here():
        return pltpu.make_async_copy(kv_ref.at[kc], kvbuf.at[z, mine], first_recv.at[mine])

    for dy, dk in ((1, 0), (1, 1), (0, 1)):
        first(dy, dk).start()

    @pl.when(shift == 0)
    def _():
        first_here().start()

    @pl.when(shift != 0)
    def _():
        first(0, 0).start()

    def q_copy(dx, dk):
        ox, tk = (lax.rem(x + dx, xs), lax.rem(kc + dk, 2))
        return remote(
            q_ref.at[tk],
            qbuf.at[x, kc],
            q_send.at[2 * dx + dk],
            q_recv.at[2 * x + kc],
            x=ox,
            core=tk,
        )

    q_here = pltpu.make_async_copy(q_ref.at[kc], qbuf.at[x, kc], q_recv.at[2 * x + kc])
    q_here.start()
    q_order = [
        (dx, dk)
        for dx in [0] + sorted(range(1, xs), key=lambda d: min(d, xs - d))
        for dk in (0, 1)
        if dx or dk
    ]
    for dx, dk in q_order:
        q_copy(dx, dk).start()

    def first_wait(s):
        remote(
            kv_ref.at[0], kvbuf.at[z, s], first_send.at[0], first_recv.at[s], z=up
        ).wait_recv()

    def ring(going_up, slot, t, h):
        send, recv, to = (up_send, up_recv, up) if going_up else (down_send, down_recv, down)
        part = kvbuf.at[slot, pl.ds(2 * h, 2)]
        return remote(part, part, send.at[t, h], recv.at[t, h], z=to)

    def sent(going_up, t, h):
        slot = lax.rem(z - t + zs, zs) if going_up else lax.rem(z + t, zs)
        return ring(going_up, slot, t, h)

    def got(going_up, t, h):
        slot = lax.rem(z - 1 - t + zs, zs) if going_up else lax.rem(z + 1 + t, zs)
        return ring(going_up, slot, t, h)

    full = (zs - 2) // 2
    for t in range(full):
        for h in range(2):
            if t == 0:
                first_wait(2 * h)
                first_wait(2 * h + 1)
            for going_up in (True, False):
                if t > 0:
                    got(going_up, t - 1, h).wait_recv()
                sent(going_up, t, h).start()
    if full == 0:
        for s in range(4):
            first_wait(s)
    for going_up, h in ((True, 0), (False, 1)):
        if full > 0:
            got(going_up, full - 1, h).wait_recv()
        sent(going_up, full, h).start()
    if full > 0:
        got(True, full - 1, 1).wait_recv()
        got(False, full - 1, 0).wait_recv()
    got(True, full, 0).wait_recv()
    got(False, full, 1).wait_recv()

    for t in range(full):
        for h in range(2):
            for going_up in (True, False):
                sent(going_up, t, h).wait_send()
    sent(True, full, 0).wait_send()
    sent(False, full, 1).wait_send()
    for dy, dk in ((1, 0), (1, 1), (0, 1)):
        first(dy, dk).wait_send()

    @pl.when(shift != 0)
    def _():
        first(0, 0).wait_send()

    for dx, dk in q_order:
        q_copy(dx, dk).wait_send()
    for s in range(2 * xs):
        remote(
            q_ref.at[0], qbuf.at[s // 2, s % 2], q_send.at[0], q_recv.at[s], z=up
        ).wait_recv()


def exchange(sizes, kv, q):
    xs, zs = sizes
    tok = q.shape[1]
    full = (zs - 2) // 2
    dma = pltpu.SemaphoreType.DMA
    return pl.pallas_call(
        functools.partial(exchange_kernel, sizes),
        out_shape=(
            jax.ShapeDtypeStruct((zs, 4, *kv.shape[1:]), kv.dtype),
            jax.ShapeDtypeStruct((xs, 2, *q.shape[1:]), q.dtype),
        ),
        in_specs=[pl.BlockSpec(memory_space=VMEM)] * 2,
        out_specs=(pl.BlockSpec(memory_space=VMEM),) * 2,
        scratch_shapes=[
            dma((4,)),
            dma((4,)),
            dma((full + 1, 2)),
            dma((full + 1, 2)),
            dma((full + 1, 2)),
            dma((full + 1, 2)),
            dma((2 * xs,)),
            dma((2 * xs,)),
        ],
        compiler_params=pltpu.CompilerParams(
            collective_id=0, has_side_effects=True, vmem_limit_bytes=24 << 20
        ),
        name="exchange",
    )(kv, q)


def flash_kernel(docs, chunks, meta, q_ref, kv_ref, o_ref, l_ref, acc, top, causal, start, order):
    xq = pl.program_id(0)
    tok = q_ref.shape[2]
    rows = 2 * tok
    heads = q_ref.shape[3] // HEAD_SIZE
    first = meta[xq]
    lanes = lax.broadcasted_iota(jnp.int32, (rows, 128), 1)
    positions = first + lax.broadcasted_iota(jnp.int32, (rows, 128), 0)
    begins = jnp.zeros((rows, 128), jnp.int32)
    low = jnp.int32(0)
    for d in range(docs):
        doc_start = meta[8 + d]
        begins = jnp.where(positions >= doc_start, jnp.maximum(begins, doc_start), begins)
        low = jnp.where(first >= doc_start, jnp.maximum(low, doc_start), low)
    causal[...] = positions - lanes
    start[...] = begins - lanes
    acc[...] = jnp.zeros_like(acc)
    top[...] = jnp.full_like(top, NEG)

    def pick(i, n):
        base = meta[32 + i]
        order[n] = i
        return n + jnp.where((base < first + rows) & (base + rows > low), 1, 0)

    active = lax.fori_loop(0, chunks, pick, jnp.int32(0))

    def step(pair, carry):
        one = order[2 * pair]
        whole = 2 * pair + 1 < active
        two = jnp.where(whole, order[2 * pair + 1], one)
        bases = (meta[32 + one], jnp.where(whole, meta[32 + two], 1 << 28))
        keys, values, biases = [], [], []
        for chunk, base in zip((one, two), bases):
            zz, yy = (chunk // 2, lax.rem(chunk, 2))
            for k in range(2):
                keys.append(kv_ref[zz, 2 * yy + k, 0])
                values.append(kv_ref[zz, 2 * yy + k, 1])
                at = base + k * tok
                ok = (causal[...] >= at) & (start[...] <= at)
                biases.append(jnp.where(ok, 0.0, NEG))
        key = jnp.concatenate(keys, axis=0)
        value = jnp.concatenate(values, axis=0)
        value = jnp.concatenate([value, jnp.ones_like(value)], axis=1)
        bias = jnp.concatenate(biases, axis=1)
        for h in range(heads):
            cols = slice(h * HEAD_SIZE, (h + 1) * HEAD_SIZE)
            q = q_ref[0, :, :, cols].reshape(rows, HEAD_SIZE)
            s = lax.dot_general(
                q, key, (((1,), (1,)), ((), ())), preferred_element_type=jnp.float32
            )
            s = s * SCALE + bias
            old = top[h]
            new = jnp.maximum(old, jnp.max(s, axis=1, keepdims=True))
            w = jnp.exp2(s - new[:, :1]).astype(jnp.bfloat16)
            update = jnp.dot(w, value, preferred_element_type=jnp.float32)
            shrink = jnp.exp2(old - new)
            top[h] = new
            acc[h] = acc[h] * jnp.concatenate([shrink, shrink], axis=1) + update
        return carry

    lax.fori_loop(0, (active + 1) // 2, step, 0)

    lane = lax.broadcasted_iota(jnp.int32, (rows, 128), 1)
    packed = jnp.full((rows, 128), NEG, jnp.float32)
    for h in range(heads):
        total = jnp.maximum(acc[h, :, HEAD_SIZE:], 1e-30)
        out = acc[h, :, :HEAD_SIZE] / total
        o_ref[0, :, :, h * HEAD_SIZE : (h + 1) * HEAD_SIZE] = out.astype(jnp.bfloat16).reshape(
            2, tok, HEAD_SIZE
        )
        packed = jnp.where(lane == h, top[h] + jnp.log2(total), packed)
    for k in range(2):
        l_ref[0, k] = jnp.transpose(packed[k * tok : (k + 1) * tok])[:8]


def flash(docs, meta, q, kv):
    xs, _, tok, width = q.shape
    chunks = kv.shape[0] * 2
    heads = width // HEAD_SIZE
    keys = kv.shape[0] * 4 * tok
    rows = 2 * tok
    return pl.pallas_call(
        functools.partial(flash_kernel, docs, chunks),
        out_shape=(
            jax.ShapeDtypeStruct(q.shape, jnp.bfloat16),
            jax.ShapeDtypeStruct((xs, 2, 8, 128), jnp.float32),
        ),
        grid=(xs,),
        in_specs=[
            pl.BlockSpec(memory_space=pltpu.SMEM),
            pl.BlockSpec((1, 2, tok, width), lambda i: (i, 0, 0, 0)),
            pl.BlockSpec(memory_space=VMEM),
        ],
        out_specs=(
            pl.BlockSpec((1, 2, tok, width), lambda i: (i, 0, 0, 0)),
            pl.BlockSpec((1, 2, 8, 128), lambda i: (i, 0, 0, 0)),
        ),
        scratch_shapes=[
            VMEM((heads, rows, 2 * HEAD_SIZE), jnp.float32),
            VMEM((heads, rows, 128), jnp.float32),
            VMEM((rows, 128), jnp.int32),
            VMEM((rows, 128), jnp.int32),
            pltpu.SMEM((chunks + 2,), jnp.int32),
        ],
        compiler_params=pltpu.CompilerParams(vmem_limit_bytes=32 << 20),
        cost_estimate=pl.CostEstimate(
            flops=4 * heads * xs * rows * keys * HEAD_SIZE // 3,
            bytes_accessed=4 << 20,
            transcendentals=heads * xs * rows * keys // 3,
        ),
        name="flash",
    )(meta, q, kv)


def rows_kernel(
    sizes,
    width_full,
    o_ref,
    l_ref,
    res_ref,
    scored_ref,
    gain_ref,
    ow_ref,
    att_ref,
    g_ref,
    obuf,
    lbuf,
    rbuf,
    cbuf,
    wbuf,
    psend,
    pbuf,
    sqbuf,
    ubuf,
    w_sem,
    o_send,
    o_recv,
    l_send,
    l_recv,
    r_send,
    r_recv,
    c_send,
    c_recv,
    p_sem,
    s_send,
    s_recv,
    u_sem,
    y_sem,
    z_send,
    z_recv,
    x_send,
    x_recv,
    k_send,
    k_recv,
):
    xs, zs = sizes
    x, yh, z, kc = (lax.axis_index(n) for n in CTX)
    hd = lax.axis_index("head")
    oy, ok, oh = (lax.rem(yh + 1, 2), lax.rem(kc + 1, 2), lax.rem(hd + 1, 2))
    row_slot = 2 * yh + kc
    quarter = 2 * kc + yh
    half = width_full // 2
    wide = half // 4

    peers = []
    for dx in range(xs):
        for dk in range(2):
            if dx or dk:
                peers.append({"x": lax.rem(x + dx, xs), "core": lax.rem(kc + dk, 2)})
    peers += [{"yh": oy}, {"yh": oy, "core": ok}]
    for where in ({}, {"core": ok}, {"yh": oy}, {"yh": oy, "core": ok}):
        peers.append({"head": oh, **where})
    for dz in range(1, zs):
        peers.append({"z": lax.rem(z + dz, zs)})

    weights = []
    for j, side in enumerate((hd, oh)):
        col = pl.multiple_of(side * half + quarter * wide, 128)
        weights.append(
            pltpu.make_async_copy(ow_ref.at[:, pl.ds(col, wide)], wbuf.at[j], w_sem.at[j])
        )
        weights[-1].start()
    greet(peers)

    o_order = [
        (dx, dk)
        for dx in sorted(range(1, xs), key=lambda d: -min(d, xs - d)) + [0]
        for dk in (0, 1)
        if dx or dk
    ]

    def o_copies(dx, dk):
        tx, tk = (lax.rem(x + dx, xs), lax.rem(kc + dk, 2))
        where = {"x": tx, "core": tk}
        s, mine = (2 * dx + dk, 2 * x + kc)
        return (
            remote(l_ref.at[tx, tk], lbuf.at[x, kc], l_send.at[s], l_recv.at[mine], **where),
            remote(o_ref.at[tx, tk], obuf.at[x, kc], o_send.at[s], o_recv.at[mine], **where),
        )

    for dx, dk in o_order:
        for copy in o_copies(dx, dk):
            copy.start()
    pltpu.make_async_copy(o_ref.at[x, kc], obuf.at[x, kc], o_recv.at[2 * x + kc]).start()
    pltpu.make_async_copy(l_ref.at[x, kc], lbuf.at[x, kc], l_recv.at[2 * x + kc]).start()

    def r_copy(dy, dk):
        ty, tk = (lax.rem(yh + dy, 2), lax.rem(kc + dk, 2))
        return remote(
            res_ref.at[2 * tk + ty],
            rbuf.at[row_slot],
            r_send.at[2 * dy + dk],
            r_recv.at[row_slot],
            yh=ty,
            core=tk,
        )

    near = ((0, 1), (1, 0), (1, 1))
    for dy, dk in near:
        r_copy(dy, dk).start()
    pltpu.make_async_copy(res_ref.at[quarter], rbuf.at[row_slot], r_recv.at[row_slot]).start()

    for s in range(2 * xs):
        at = (s // 2, s % 2)
        remote(l_ref.at[0, 0], lbuf.at[at], l_send.at[0], l_recv.at[s], head=oh).wait_recv()
        remote(o_ref.at[0, 0], obuf.at[at], o_send.at[0], o_recv.at[s], head=oh).wait_recv()

    for k in range(2):
        parts = [lbuf[j, k] for j in range(xs)]
        highest = functools.reduce(jnp.maximum, parts)
        parts = [jnp.exp2(part - highest) for part in parts]
        total = functools.reduce(jnp.add, parts)
        parts = [part / total for part in parts]
        padding = [jnp.zeros((128 - 8 * xs, 128), jnp.float32)]
        shares = jnp.transpose(jnp.concatenate(parts + padding, axis=0))
        heads = o_ref.shape[3] // HEAD_SIZE
        for h in range(heads):
            cols = slice(h * HEAD_SIZE, (h + 1) * HEAD_SIZE)
            merged = sum(
                shares[:, 8 * j + h : 8 * j + h + 1] * obuf[j, k, :, cols].astype(jnp.float32)
                for j in range(xs)
            )
            out = (k * heads + h) * HEAD_SIZE
            att_ref[:, out : out + HEAD_SIZE] = merged.astype(jnp.bfloat16)

    tok = att_ref.shape[0]
    hot = scored_ref[...] == lax.broadcasted_iota(jnp.int32, (16, tok), 1)
    hot = jnp.where(hot, 1.0, 0.0).astype(jnp.bfloat16)
    cbuf[row_slot] = jnp.dot(hot, att_ref[...], preferred_element_type=jnp.float32).astype(
        jnp.bfloat16
    )

    def c_copy(dy, dk):
        return remote(
            cbuf.at[row_slot],
            cbuf.at[row_slot],
            c_send.at[2 * dy + dk],
            c_recv.at[2 * dy + dk],
            yh=lax.rem(yh + dy, 2),
            core=lax.rem(kc + dk, 2),
        )

    for dy, dk in near:
        c_copy(dy, dk).start()
    for dy, dk in near:
        c_copy(dy, dk).wait_recv()
    for copy in weights:
        copy.wait()
    chosen = (cbuf[0] + cbuf[1]) + (cbuf[2] + cbuf[3])
    psend[...] = jnp.dot(chosen, wbuf[1], preferred_element_type=jnp.float32).astype(jnp.bfloat16)
    p_copy = remote(psend, pbuf, p_sem.at[0], p_sem.at[1], head=oh)
    p_copy.start()
    hidden = jnp.dot(chosen, wbuf[0], preferred_element_type=jnp.float32)
    for s in range(4):
        remote(res_ref.at[0], rbuf.at[s], r_send.at[0], r_recv.at[s], head=oh).wait_recv()
    residual = (rbuf[0] + rbuf[1]) + (rbuf[2] + rbuf[3])
    p_copy.wait_recv()
    hidden = residual.astype(jnp.float32) + (hidden + pbuf[...].astype(jnp.float32))

    own = 4 * hd + row_slot
    sqbuf[own] = jnp.broadcast_to(jnp.sum(hidden * hidden, axis=1, keepdims=True), (16, 128))

    def s_copy(d):
        dh, dy, dk = (d // 4, d // 2 % 2, d % 2)
        return remote(
            sqbuf.at[own],
            sqbuf.at[own],
            s_send.at[d],
            s_recv.at[d],
            head=lax.rem(hd + dh, 2),
            yh=lax.rem(yh + dy, 2),
            core=lax.rem(kc + dk, 2),
        )

    for d in range(1, 8):
        s_copy(d).start()
    for d in range(1, 8):
        s_copy(d).wait_recv()
    squares = functools.reduce(jnp.add, [sqbuf[s] for s in range(8)])
    scale = lax.rsqrt(squares / width_full + 1e-05)[:, :1]
    ubuf[...] = (hidden * scale * gain_ref[quarter]).astype(jnp.bfloat16)

    mine = pl.ds(pl.multiple_of(quarter * wide, 128), wide)
    both = pl.ds(pl.multiple_of(kc * 2 * wide, 128), 2 * wide)
    others = pl.ds(pl.multiple_of(ok * 2 * wide, 128), 2 * wide)
    here = pltpu.make_async_copy(ubuf, g_ref.at[x, z, :, mine], u_sem)
    here.start()
    y_copy = remote(ubuf, g_ref.at[x, z, :, mine], y_sem.at[0], y_sem.at[1], yh=oy)
    y_copy.start()
    here.wait()
    y_copy.wait_recv()

    def block(bx, bz):
        return g_ref.at[bx, bz, :, both]

    def z_copy(dz):
        to = lax.rem(z + dz, zs)
        return remote(block(x, z), block(x, z), z_send.at[dz], z_recv.at[dz], z=to)

    def x_copy(dx, dz):
        bz = lax.rem(z + zs - dz, zs)
        to = lax.rem(x + dx, xs)
        return remote(block(x, bz), block(x, bz), x_send.at[dx, dz], x_recv.at[dx, dz], x=to)

    def k_copy(dx):
        plane = g_ref.at[lax.rem(x + xs - dx, xs), :, :, both]
        return remote(plane, plane, k_send.at[dx], k_recv.at[dx], core=ok)

    z_order = sorted(range(1, zs), key=lambda d: min(d, zs - d))
    x_order = sorted(range(1, xs), key=lambda d: min(d, xs - d))
    for dz in reversed(z_order):
        z_copy(dz).start()
    for dz in [0] + z_order:
        if dz:
            z_copy(dz).wait_recv()
        for dx in x_order:
            x_copy(dx, dz).start()
    k_copy(0).start()
    for dx in x_order:
        for dz in [0] + z_order:
            x_copy(dx, dz).wait_recv()
        k_copy(dx).start()
    for dx in range(xs):
        k_copy(dx).wait_recv()

    for dx, dk in o_order:
        for copy in o_copies(dx, dk):
            copy.wait_send()
    for dy, dk in near:
        r_copy(dy, dk).wait_send()
        c_copy(dy, dk).wait_send()
    p_copy.wait_send()
    for d in range(1, 8):
        s_copy(d).wait_send()
    y_copy.wait_send()
    for dz in z_order:
        z_copy(dz).wait_send()
    for dx in x_order:
        for dz in range(zs):
            x_copy(dx, dz).wait_send()
    for dx in range(xs):
        k_copy(dx).wait_send()


def gathered_rows(sizes, o, l, res, scored, gain, out_weight):
    xs, zs = sizes
    tok = o.shape[2]
    width_full = out_weight.shape[1]
    depth = out_weight.shape[0]
    half = width_full // 2
    wide = half // 4
    dma = pltpu.SemaphoreType.DMA
    bf16 = jnp.bfloat16
    return pl.pallas_call(
        functools.partial(rows_kernel, sizes, width_full),
        out_shape=(
            jax.ShapeDtypeStruct((tok, depth), bf16),
            jax.ShapeDtypeStruct((xs, zs, 16, half), bf16),
        ),
        in_specs=[pl.BlockSpec(memory_space=VMEM)] * 5 + [pl.BlockSpec(memory_space=pl.ANY)],
        out_specs=(pl.BlockSpec(memory_space=VMEM),) * 2,
        scratch_shapes=[
            VMEM(o.shape, bf16),
            VMEM(l.shape, jnp.float32),
            VMEM((4, 16, wide), bf16),
            VMEM((4, 16, depth), bf16),
            VMEM((2, depth, wide), bf16),
            VMEM((16, wide), bf16),
            VMEM((16, wide), bf16),
            VMEM((8, 16, 128), jnp.float32),
            VMEM((16, wide), bf16),
            dma((2,)),
            dma((2 * xs,)),
            dma((2 * xs,)),
            dma((2 * xs,)),
            dma((2 * xs,)),
            dma((4,)),
            dma((4,)),
            dma((4,)),
            dma((4,)),
            dma((2,)),
            dma((8,)),
            dma((8,)),
            dma,
            dma((2,)),
            dma((zs,)),
            dma((zs,)),
            dma((xs, zs)),
            dma((xs, zs)),
            dma((xs,)),
            dma((xs,)),
        ],
        compiler_params=pltpu.CompilerParams(
            collective_id=1, has_side_effects=True, vmem_limit_bytes=32 << 20
        ),
        name="gathered_rows",
    )(o, l, res, scored, gain, out_weight)


def stats_kernel(
    sizes,
    logits_ref,
    ids_ref,
    out_ref,
    lbuf,
    kbuf,
    ybuf,
    xbuf,
    zbuf,
    e_sem,
    k_sem,
    y_sem,
    x_send,
    x_recv,
    z_send,
    z_recv,
    h_sem,
):
    xs, zs = sizes
    x, yh, z, kc = (lax.axis_index(n) for n in CTX)
    hd = lax.axis_index("head")
    oy, ok, oh = (lax.rem(yh + 1, 2), lax.rem(kc + 1, 2), lax.rem(hd + 1, 2))
    peers = [{"head": oh}, {"core": ok}, {"yh": oy}]
    for dx in range(1, xs):
        peers.append({"x": lax.rem(x + dx, xs)})
    for dz in range(1, zs):
        peers.append({"z": lax.rem(z + dz, zs)})
    greet(peers)

    e_copy = remote(logits_ref.at[oh], lbuf, e_sem.at[0], e_sem.at[1], head=oh)
    e_copy.start()
    e_copy.wait_recv()

    rows, width = lbuf.shape
    tile = min(128, rows)
    for at in range(0, rows, tile):
        span = slice(at, at + tile)
        logits = logits_ref[hd, span].astype(jnp.float32) + lbuf[span].astype(jnp.float32)
        highest = jnp.max(logits, axis=1, keepdims=True)
        total = jnp.sum(jnp.exp(logits - highest), axis=1, keepdims=True)
        match = ids_ref[span] == lax.broadcasted_iota(jnp.int32, (tile, width), 1)
        target = jnp.sum(jnp.where(match, logits, 0.0), axis=1, keepdims=True)
        lane = lax.broadcasted_iota(jnp.int32, (tile, 128), 1)
        packed = jnp.where(lane == 0, highest, jnp.where(lane == 1, total, target))
        kbuf[kc, :, at : at + tile] = jnp.transpose(packed)[:8]

    def merge(buf, count):
        tops = [buf[i, 0:1] for i in range(count)]
        top = functools.reduce(jnp.maximum, tops)
        total = functools.reduce(
            jnp.add, [buf[i, 1:2] * jnp.exp(tops[i] - top) for i in range(count)]
        )
        target = functools.reduce(jnp.add, [buf[i, 2:3] for i in range(count)])
        return jnp.concatenate([top, total] + [target] * 6, axis=0)

    k_copy = remote(kbuf.at[kc], kbuf.at[kc], k_sem.at[0], k_sem.at[1], core=ok)
    k_copy.start()
    k_copy.wait_recv()
    ybuf[yh] = merge(kbuf, 2)
    y_copy = remote(ybuf.at[yh], ybuf.at[yh], y_sem.at[0], y_sem.at[1], yh=oy)
    y_copy.start()
    y_copy.wait_recv()
    xbuf[x] = merge(ybuf, 2)

    def x_copy(d):
        to = lax.rem(x + d, xs)
        return remote(xbuf.at[x], xbuf.at[x], x_send.at[d], x_recv.at[d], x=to)

    for d in range(1, xs):
        x_copy(d).start()
    for d in range(1, xs):
        x_copy(d).wait_recv()
    zbuf[z] = merge(xbuf, xs)

    def z_copy(d):
        to = lax.rem(z + d, zs)
        return remote(zbuf.at[z], zbuf.at[z], z_send.at[d], z_recv.at[d], z=to)

    for d in range(1, zs):
        z_copy(d).start()
    for d in range(1, zs):
        z_copy(d).wait_recv()
    final = merge(zbuf, zs)
    out_ref[hd] = jnp.broadcast_to(final[2:3] - final[0:1] - jnp.log(final[1:2]), final.shape)
    h_copy = remote(out_ref.at[hd], out_ref.at[hd], h_sem.at[0], h_sem.at[1], head=oh)
    h_copy.start()
    h_copy.wait_recv()

    e_copy.wait_send()
    k_copy.wait_send()
    y_copy.wait_send()
    for d in range(1, xs):
        x_copy(d).wait_send()
    for d in range(1, zs):
        z_copy(d).wait_send()
    h_copy.wait_send()


def row_stats(sizes, logits, ids):
    xs, zs = sizes
    _, rows, width = logits.shape
    dma = pltpu.SemaphoreType.DMA
    f32 = jnp.float32
    return pl.pallas_call(
        functools.partial(stats_kernel, sizes),
        out_shape=jax.ShapeDtypeStruct((2, 8, rows), f32),
        in_specs=[pl.BlockSpec(memory_space=VMEM)] * 2,
        out_specs=pl.BlockSpec(memory_space=VMEM),
        scratch_shapes=[
            VMEM((rows, width), jnp.bfloat16),
            VMEM((2, 8, rows), f32),
            VMEM((2, 8, rows), f32),
            VMEM((xs, 8, rows), f32),
            VMEM((zs, 8, rows), f32),
            dma((2,)),
            dma((2,)),
            dma((2,)),
            dma((xs,)),
            dma((xs,)),
            dma((zs,)),
            dma((zs,)),
            dma((2,)),
        ],
        compiler_params=pltpu.CompilerParams(
            collective_id=2, has_side_effects=True, vmem_limit_bytes=24 << 20
        ),
        name="row_stats",
    )(logits, ids)


def per_device(
    sizes,
    queries,
    rotated_keys,
    value_matrix,
    doc_lengths,
    scored,
    residual,
    norm_gain,
    out_weight,
    lm_weight,
    token_ids,
    old_logp,
    advantage,
):
    xs, zs = sizes
    tok = queries.shape[0]
    x, yh, z, kc = (lax.axis_index(n) for n in CTX)
    hd = lax.axis_index("head")
    docs = doc_lengths.shape[0]
    plane = 4 * zs * tok

    kv = jnp.stack([rotated_keys, value_matrix]).reshape(2, tok, 2, HEAD_SIZE)
    kv = jnp.transpose(kv, (2, 0, 1, 3))
    q = jnp.transpose(queries.reshape(tok, 2, -1), (1, 0, 2))
    kvs, qs = exchange(sizes, kv, q)

    block = yh * zs + z
    doc_starts = jnp.cumsum(doc_lengths) - doc_lengths
    q_first = jnp.arange(8, dtype=jnp.int32) * plane + block * 2 * tok
    zz = jnp.arange(zs, dtype=jnp.int32)[:, None]
    yy = jnp.arange(2, dtype=jnp.int32)[None, :]
    source_x = (x - zz + 2 * xs * zs) % xs
    bases = source_x * plane + (yy * zs + zz) * 2 * tok
    meta = jnp.concatenate(
        [q_first, jnp.pad(doc_starts.astype(jnp.int32), (0, 24 - docs)), bases.reshape(-1)]
    )
    o, l = flash(docs, meta, qs, kvs)

    row_slot = 2 * yh + kc
    resp = scored.shape[0]
    mine = (jnp.arange(4, dtype=jnp.int32) == row_slot)[:, None]
    scored16 = jnp.where(mine, scored[None, :], -1).reshape(4 * resp, 1)
    half = residual.shape[1]
    res = jnp.where(mine[:, :, None], residual[None], 0).astype(jnp.bfloat16)
    res = jnp.transpose(res.reshape(4 * resp, 4, half // 4), (1, 0, 2))
    gain = norm_gain.reshape(4, 1, half // 4)
    attended, rows = gathered_rows(sizes, o, l, res, scored16, gain, out_weight)

    count = xs * zs * 4 * resp
    logits = jnp.dot(
        rows.reshape(count, half), lm_weight, preferred_element_type=jnp.float32
    ).astype(jnp.bfloat16)
    vocab = lm_weight.shape[1]
    start = (((x * 2 + yh) * zs + z) * 2 + kc) * vocab
    ids = token_ids.reshape(xs, 2, zs, 2, resp).transpose(0, 2, 1, 3, 4).reshape(2, count // 2)
    ids = lax.dynamic_index_in_dim(ids, hd, 0, keepdims=False)[:, None] - start
    found = row_stats(sizes, logits.reshape(2, count // 2, vocab), ids)
    log_probs = found[:, 0].reshape(xs, zs, 2, 2, resp).transpose(0, 2, 1, 3, 4).reshape(count)
    ratio = jnp.exp(jnp.clip(log_probs - old_logp, -4.0, 4.0))
    token_loss = -jnp.minimum(ratio * advantage, jnp.clip(ratio, 0.8, 1.2) * advantage)
    return (attended, log_probs, token_loss)


def solution(mesh, shape=(4, 2, 8, 2)):
    finer = Mesh(mesh.devices.reshape(*shape, mesh.shape["head"]), NAMES)
    placed = (
        P(CTX, "head"),
        P(CTX, "head"),
        P(CTX, "head"),
        P(),
        P(CTX),
        P(CTX, "head"),
        P("head"),
        P("head", None),
        P("head", CTX),
        P(),
        P(),
        P(),
    )
    return jax.shard_map(
        functools.partial(per_device, (shape[0], shape[2])),
        mesh=finer,
        in_specs=placed,
        out_specs=(P(CTX, "head"), P(), P()),
        check_vma=False,
    )
```

time: 493 us -> 163 us (0.33)
  waiting for transfers between devices: 264 us -> 0 us
  Pallas kernels: 0 us -> 147 us
  blocking collectives: 60 us -> 0 us
  matrix products: 56.6 us -> 2.33 us
  local copies, waits for them, and re-layouts: 53.7 us -> 9.32 us
  other arithmetic: 34.7 us -> 2.43 us
  between operations: 14.3 us -> 0.9 us
  starting transfers between devices: 5.08 us -> 0 us
    all_gather x2 -> x0, waiting for transfers between devices: 251 us -> none  [the longest x1 136 us: side_by_side(): whole, at, outs = (lax.all_gather(both, axis, axis=dim, tiled=True), 0, [])]
    pallas_call x0 -> x4, Pallas kernels: none -> 147 us  [the longest x1 63.6 us: gathered_rows(): pl.pallas_call(functools.partial(rows_kernel, sizes, width_full), out_sha...]
    dot_general x66 -> x1, matrix products: 56.6 us -> 2.33 us  [per_device(): jnp.dot(rows.reshape(count, half), lm_weight, preferred_element_type=jnp....]
    all_gather x5 -> x0, blocking collectives: 48.9 us -> none  [all_in_one(): both, at, found = (lax.all_gather(jnp.concatenate(lines), axis), 0, {})]
    dynamic_slice x32 -> x0, local copies, waits for them, and re-layouts: 34.3 us -> none  [one_block(): value_part = lax.dynamic_slice_in_dim(value_rows, start_row, block_rows, 0)]
    reduce_sum x70 -> x0, other arithmetic: 20.2 us -> none  [the longest x32 16.7 us: attend_rows(): row_total = row_total * rescale + jnp.sum(weights, axis=-1)]
    all_to_all x1 -> x0, waiting for transfers between devices: 12.3 us -> none  [sum_at_owner(): lax.all_to_all(pieces, axis, split_axis=0, concat_axis=0, tiled=True)]
    slice x1, local copies, waits for them, and re-layouts: 11.4 us -> 0.02 us  [per_device(): found[:, 0].reshape(xs, zs, 2, 2, resp).transpose(0, 2, 1, 3, 4)]
  transfers between devices with their start and end apart: 3 -> 0, of which waited for: 3 -> 0; matrix products, arithmetic and copies ran while one was open for 1% -> 0% of each run, Pallas kernels for 0% -> 0%
where the time goes in v1:
time: 163 us; the launch traced here: 162 us
  Pallas kernels  147 us (90%)
  local copies, waits for them, and re-layouts  9.32 us (6%)
  other arithmetic  2.43 us (1%)
  matrix products  2.33 us (1%)
    pallas_call x1, Pallas kernels, gathered_rows(): pl.pallas_call(functools.partial(rows_kernel, sizes, width_full), out_sha...  63.6 us
    pallas_call x1, Pallas kernels, exchange(): pl.pallas_call(functools.partial(exchange_kernel, sizes), out_shape=(jax....  39.4 us
    pallas_call x1, Pallas kernels, row_stats(): pl.pallas_call(functools.partial(stats_kernel, sizes), out_shape=jax.Shap...  31.1 us
    pallas_call x1, Pallas kernels, flash(): pl.pallas_call(functools.partial(flash_kernel, docs, chunks), out_shape=(...  12.7 us
    unnamed x22, local copies, waits for them, and re-layouts  7.25 us

profile of v1, /device:TPU:8, one launch (start us, length us, event | category | flops | bytes accessed | tf_op | source)
XLA Modules:
  0.0 161.7 jit_solution(6585042212337819960)
XLA Ops:
  0.6 0.8 reduce-window.9
  1.5 0.7 bitcast_subtract_fusion
  2.4 1.1 copy.21
  3.5 0.1 copy.22
  3.7 1.0 copy.17
  4.6 0.1 copy.19
  4.8 1.0 copy.18
  5.7 0.1 copy.20
  5.9 39.4 %exchange.1 = (bf16[8,4,2,128,128]{4,3,2,1,0:T(8,128)(2,1)S(1)}, bf16[4,2,128,512]{3,2,1,0:T(8,128)(2,1)S(1)}) custom-call(bf16[2,2,128,128]{3,2,1,0:T(8,128)(2,1)S(1)} %maximum_bitcast_fusion.kv_ref, bf16[2,128,512]{2,1,0:T(8,128)(2,1)S(1)} %bitcast.21), custom_call_target="tpu_custom_call" | custom-call | tf_op jit(solution)/shard_map/exchange/pallas_call | solution.py:191
  45.3 12.7 %flash.1 = (bf16[4,2,128,512]{3,2,1,0:T(8,128)(2,1)S(1)}, f32[4,2,8,128]{3,2,1,0:T(8,128)S(1)}) custom-call(s32[48]{0:T(128)S(1)} %fusion.3.meta, bf16[4,2,128,512]{3,2,1,0:T(8,128)(2,1)S(1)} %get-tuple-element.9.q_ref, bf16[8,4,2,128,128]{4,3,2,1,0:T(8,128)(2,1)S(1)} %get-tuple-element.10.kv_ref), custom_call_target="tpu_custom_call" | custom-call | flops 2863311616 | bytes 4194304 | tf_op jit(solution)/shard_map/flash/pallas_call | solution.py:297
  58.1 0.1 broadcast_in_dim.51
  58.5 3.4 %copy-done = bf16[1024,4096]{1,0:T(8,128)(2,1)S(1)} copy-done((bf16[1024,4096]{1,0:T(8,128)(2,1)S(1)}, bf16[1024,4096]{1,0:T(8,128)(2,1)}, u32[]{:S(2)}) %copy-start) | copy-done | bytes 8388632
  61.9 63.6 %gathered_rows.1 = (bf16[128,1024]{1,0:T(8,128)(2,1)S(1)}, bf16[4,8,16,2048]{3,2,1,0:T(8,128)(2,1)S(1)}) custom-call(bf16[4,2,128,512]{3,2,1,0:T(8,128)(2,1)S(1)} %get-tuple-element.11.o_ref, f32[4,2,8,128]{3,2,1,0:T(8,128)S(1)} %get-tuple-element.12.l_ref, bf16[4,16,512]{2,1,0:T(8,128)(2,1)S(1)} %fusion.res_ref, s32[16,1]{1,0:T(8,128)S(1)} %select_n.40.scored_ref, ...), custom_call_target="tpu_custom_call" | custom-call | tf_op jit(solution)/shard_map/gathered_rows/pallas_call | solution.py:589
  125.5 2.3 %convolution_convert_fusion = bf16[512,1002]{0,1:T(8,128)(2,1)S(1)} fusion(bf16[512,2048]{1,0:T(8,128)(2,1)S(1)} %bitcast.23, bf16[2048,1002]{0,1:T(8,128)(2,1)S(1)} %copy-done.8), kind=kOutput, calls=%fused_computation | convolution fusion | flops 2101859328 | bytes 7227392 | tf_op jit(solution)/shard_map/dot_general | solution.py:816
  127.8 0.5 copy.25
  128.4 0.1 copy-done.4
  128.5 0.1 reshape.155
  128.7 0.1 reshape.156
  128.8 0.1 copy.27.ids_ref
  128.9 31.1 %row_stats.1 = f32[2,8,256]{2,1,0:T(8,128)S(1)} custom-call(bf16[2,256,1002]{2,1,0:T(8,128)(2,1)S(1)} %bitcast.20, s32[256,1]{1,0:T(8,128)S(1)} %copy.27.ids_ref), custom_call_target="tpu_custom_call" | custom-call | tf_op jit(solution)/shard_map/row_stats/pallas_call | solution.py:739
  160.0 0.1 reshape_squeeze.3
  160.2 0.1 reshape.157
  160.4 0.6 minimum_negate_fusion
  161.0 0.7 copy.33
  (33 shorter events, 0.8 us)
Async XLA Ops:
  45.3 12.9 %copy-start.2 = (bf16[4,2048]{1,0:T(4,128)(2,1)S(1)}, bf16[4,2048]{1,0:T(4,128)(2,1)}, u32[]{:S(2)}) copy-start(bf16[4,2048]{1,0:T(4,128)(2,1)} %param.17) | copy-start | bytes 49156
  45.3 13.0 %copy-start.7 = (s32[4]{0:T(128)S(1)}, s32[4]{0:T(128)}, u32[]{:S(2)}) copy-start(s32[4]{0:T(128)} %param.16) | copy-start | bytes 52
  45.3 13.2 %copy-start.1 = (f32[2048]{0:T(1024)S(1)}, f32[2048]{0:T(1024)}, u32[]{:S(2)}) copy-start(f32[2048]{0:T(1024)} %param.18) | copy-start | bytes 24580
  58.5 3.4 %copy-start = (bf16[1024,4096]{1,0:T(8,128)(2,1)S(1)}, bf16[1024,4096]{1,0:T(8,128)(2,1)}, u32[]{:S(2)}) copy-start(bf16[1024,4096]{1,0:T(8,128)(2,1)} %ow_ref.1) | copy-start | bytes 25165828
  61.9 63.6 %copy-start.8 = (bf16[2048,1002]{0,1:T(8,128)(2,1)S(1)}, bf16[2048,1002]{0,1:T(8,128)(2,1)}, u32[]{:S(2)}) copy-start(bf16[2048,1002]{0,1:T(8,128)(2,1)} %param.20) | copy-start | bytes 12312580
  127.8 0.7 copy-start.4
  127.8 32.6 %copy-start.5 = (f32[512]{0:T(512)S(1)}, f32[512]{0:T(512)}, u32[]{:S(2)}) copy-start(f32[512]{0:T(512)} %param.23) | copy-start | bytes 6148
  127.8 32.6 %copy-start.6 = (f32[512]{0:T(512)S(1)}, f32[512]{0:T(512)}, u32[]{:S(2)}) copy-start(f32[512]{0:T(512)} %param.22) | copy-start | bytes 6148
  160.4 1.3 copy-start.3

commit v2 on v1

v2 whole, which is shorter than its diff:
```python
import functools
import math

import jax
import jax.numpy as jnp
from jax import lax
from jax.experimental import pallas as pl
from jax.experimental.pallas import tpu as pltpu
from jax.sharding import Mesh
from jax.sharding import PartitionSpec as P

HEAD_SIZE = 128
CTX = ("x", "yh", "z", "core")
NAMES = ("x", "yh", "z", "core", "head")
NEG = -1e30
SCALE = HEAD_SIZE**-0.5 * math.log2(math.e)
MESH = pl.DeviceIdType.MESH
VMEM = pltpu.VMEM


def remote(src, dst, send_sem, recv_sem, **where):
    return pltpu.make_async_remote_copy(
        src_ref=src,
        dst_ref=dst,
        send_sem=send_sem,
        recv_sem=recv_sem,
        device_id=where,
        device_id_type=MESH,
    )


def greet(peers):
    barrier = pltpu.get_barrier_semaphore()
    for where in peers:
        pl.semaphore_signal(barrier, inc=1, device_id=where, device_id_type=MESH)
    pl.semaphore_wait(barrier, len(peers))


def exchange_kernel(
    sizes,
    k_ref,
    v_ref,
    q_ref,
    hot_ref,
    kvbuf,
    qbuf,
    hotbuf,
    first_send,
    first_recv,
    up_send,
    up_recv,
    down_send,
    down_recv,
    q_send,
    q_recv,
    h_send,
    h_recv,
):
    xs, zs = sizes
    x, yh, z, kc = (lax.axis_index(n) for n in CTX)
    up, down = (lax.rem(z + 1, zs), lax.rem(z + zs - 1, zs))
    shift = lax.rem(z, xs)
    tx = lax.rem(x + z, xs)
    mine = 2 * yh + kc
    group = q_ref.shape[1] // 2
    peers = []
    for dx in range(xs):
        for dy in range(2):
            for dk in range(2):
                if dx or dy or dk:
                    peers.append(
                        {
                            "x": lax.rem(x + dx, xs),
                            "yh": lax.rem(yh + dy, 2),
                            "core": lax.rem(kc + dk, 2),
                        }
                    )
    peers.append({"z": up})
    peers.append({"z": down})
    greet(peers)

    def columns(ref, head, width):
        return ref.at[:, pl.ds(pl.multiple_of(head * width, 128), width)]

    def first(dy, dk):
        ty, tk = (lax.rem(yh + dy, 2), lax.rem(kc + dk, 2))
        return [
            remote(
                columns(ref, tk, HEAD_SIZE),
                kvbuf.at[z, mine, i],
                first_send.at[2 * dy + dk, i],
                first_recv.at[mine, i],
                x=tx,
                yh=ty,
                core=tk,
            )
            for i, ref in enumerate((k_ref, v_ref))
        ]

    def first_here():
        return [
            pltpu.make_async_copy(
                columns(ref, kc, HEAD_SIZE), kvbuf.at[z, mine, i], first_recv.at[mine, i]
            )
            for i, ref in enumerate((k_ref, v_ref))
        ]

    for dy, dk in ((1, 0), (1, 1), (0, 1)):
        for copy in first(dy, dk):
            copy.start()

    @pl.when(shift == 0)
    def _():
        for copy in first_here():
            copy.start()

    @pl.when(shift != 0)
    def _():
        for copy in first(0, 0):
            copy.start()

    def q_copies(dx, dk):
        ox, tk = (lax.rem(x + dx, xs), lax.rem(kc + dk, 2))
        s, own = (2 * dx + dk, 2 * x + kc)
        where = {"x": ox, "core": tk}
        q_part = columns(q_ref, tk, group)
        return (
            remote(hot_ref, hotbuf.at[x, kc], h_send.at[s], h_recv.at[own], **where),
            remote(q_part, qbuf.at[x, kc], q_send.at[s], q_recv.at[own], **where),
        )

    pltpu.make_async_copy(
        columns(q_ref, kc, group), qbuf.at[x, kc], q_recv.at[2 * x + kc]
    ).start()
    pltpu.make_async_copy(hot_ref, hotbuf.at[x, kc], h_recv.at[2 * x + kc]).start()
    q_order = [
        (dx, dk)
        for dx in [0] + sorted(range(1, xs), key=lambda d: min(d, xs - d))
        for dk in (0, 1)
        if dx or dk
    ]
    for dx, dk in q_order:
        for copy in q_copies(dx, dk):
            copy.start()

    def first_wait(s):
        for i in range(2):
            part = kvbuf.at[z, s, i]
            remote(part, part, first_send.at[0, i], first_recv.at[s, i], z=up).wait_recv()

    def ring(going_up, slot, t, h):
        send, recv, to = (up_send, up_recv, up) if going_up else (down_send, down_recv, down)
        part = kvbuf.at[slot, pl.ds(2 * h, 2)]
        return remote(part, part, send.at[t, h], recv.at[t, h], z=to)

    def sent(going_up, t, h):
        slot = lax.rem(z - t + zs, zs) if going_up else lax.rem(z + t, zs)
        return ring(going_up, slot, t, h)

    def got(going_up, t, h):
        slot = lax.rem(z - 1 - t + zs, zs) if going_up else lax.rem(z + 1 + t, zs)
        return ring(going_up, slot, t, h)

    full = (zs - 2) // 2
    for t in range(full):
        for h in range(2):
            if t == 0:
                first_wait(2 * h)
                first_wait(2 * h + 1)
            for going_up in (True, False):
                if t > 0:
                    got(going_up, t - 1, h).wait_recv()
                sent(going_up, t, h).start()
    if full == 0:
        for s in range(4):
            first_wait(s)
    for going_up, h in ((True, 0), (False, 1)):
        if full > 0:
            got(going_up, full - 1, h).wait_recv()
        sent(going_up, full, h).start()
    if full > 0:
        got(True, full - 1, 1).wait_recv()
        got(False, full - 1, 0).wait_recv()
    got(True, full, 0).wait_recv()
    got(False, full, 1).wait_recv()

    for t in range(full):
        for h in range(2):
            for going_up in (True, False):
                sent(going_up, t, h).wait_send()
    sent(True, full, 0).wait_send()
    sent(False, full, 1).wait_send()
    for dy, dk in ((1, 0), (1, 1), (0, 1)):
        for copy in first(dy, dk):
            copy.wait_send()

    @pl.when(shift != 0)
    def _():
        for copy in first(0, 0):
            copy.wait_send()

    for dx, dk in q_order:
        for copy in q_copies(dx, dk):
            copy.wait_send()
    for s in range(2 * xs):
        part = qbuf.at[s // 2, s % 2]
        remote(part, part, q_send.at[0], q_recv.at[s], z=up).wait_recv()
        part = hotbuf.at[s // 2, s % 2]
        remote(part, part, h_send.at[0], h_recv.at[s], z=up).wait_recv()


def exchange(sizes, k, v, q, hot):
    xs, zs = sizes
    tok = q.shape[0]
    full = (zs - 2) // 2
    dma = pltpu.SemaphoreType.DMA
    return pl.pallas_call(
        functools.partial(exchange_kernel, sizes),
        out_shape=(
            jax.ShapeDtypeStruct((zs, 4, 2, tok, HEAD_SIZE), k.dtype),
            jax.ShapeDtypeStruct((xs, 2, tok, q.shape[1] // 2), q.dtype),
            jax.ShapeDtypeStruct((xs, 2, *hot.shape), hot.dtype),
        ),
        in_specs=[pl.BlockSpec(memory_space=VMEM)] * 4,
        out_specs=(pl.BlockSpec(memory_space=VMEM),) * 3,
        scratch_shapes=[
            dma((4, 2)),
            dma((4, 2)),
            dma((full + 1, 2)),
            dma((full + 1, 2)),
            dma((full + 1, 2)),
            dma((full + 1, 2)),
            dma((2 * xs,)),
            dma((2 * xs,)),
            dma((2 * xs,)),
            dma((2 * xs,)),
        ],
        compiler_params=pltpu.CompilerParams(
            collective_id=0, has_side_effects=True, vmem_limit_bytes=24 << 20
        ),
        name="exchange",
    )(k, v, q, hot)


def flash_kernel(
    sizes,
    docs,
    lengths,
    q_ref,
    kv_ref,
    hot_ref,
    o_ref,
    l_ref,
    co_ref,
    cl_ref,
    acc,
    top,
    causal,
    start,
    order,
    where,
):
    xs, zs = sizes
    chunks = 2 * zs
    xq = pl.program_id(0)
    x, yh, z, _ = (lax.axis_index(n) for n in CTX)
    tok = q_ref.shape[2]
    rows = 2 * tok
    plane = chunks * rows
    heads = q_ref.shape[3] // HEAD_SIZE
    first = xq * plane + (yh * zs + z) * rows
    lanes = lax.broadcasted_iota(jnp.int32, (rows, 128), 1)
    positions = first + lax.broadcasted_iota(jnp.int32, (rows, 128), 0)
    begins = jnp.zeros((rows, 128), jnp.int32)
    low = jnp.int32(0)
    doc_start = jnp.int32(0)
    for d in range(docs):
        begins = jnp.where(positions >= doc_start, doc_start, begins)
        low = jnp.where(first >= doc_start, doc_start, low)
        doc_start = doc_start + lengths[d]
    causal[...] = positions - lanes
    start[...] = begins - lanes
    acc[...] = jnp.zeros_like(acc)
    top[...] = jnp.full_like(top, NEG)

    active = jnp.int32(0)
    for i in range(chunks):
        zz, yy = (i // 2, i % 2)
        base = lax.rem(x + 2 * xs * zs - zz, xs) * plane + (yy * zs + zz) * rows
        order[active] = i
        where[active] = base
        active = active + jnp.where((base < first + rows) & (base + rows > low), 1, 0)

    def step(pair, carry):
        one = order[2 * pair]
        whole = 2 * pair + 1 < active
        two = jnp.where(whole, order[2 * pair + 1], one)
        bases = (where[2 * pair], jnp.where(whole, where[2 * pair + 1], 1 << 28))
        keys, values, biases = [], [], []
        for chunk, base in zip((one, two), bases):
            zz, yy = (chunk // 2, lax.rem(chunk, 2))
            for k in range(2):
                keys.append(kv_ref[zz, 2 * yy + k, 0])
                values.append(kv_ref[zz, 2 * yy + k, 1])
                at = base + k * tok
                ok = (causal[...] >= at) & (start[...] <= at)
                biases.append(jnp.where(ok, 0.0, NEG))
        key = jnp.concatenate(keys, axis=0)
        value = jnp.concatenate(values, axis=0)
        value = jnp.concatenate([value, jnp.ones_like(value)], axis=1)
        bias = jnp.concatenate(biases, axis=1)
        for h in range(heads):
            cols = slice(h * HEAD_SIZE, (h + 1) * HEAD_SIZE)
            q = q_ref[0, :, :, cols].reshape(rows, HEAD_SIZE)
            s = lax.dot_general(
                q, key, (((1,), (1,)), ((), ())), preferred_element_type=jnp.float32
            )
            s = s * SCALE + bias
            old = top[h]
            new = jnp.maximum(old, jnp.max(s, axis=1, keepdims=True))
            w = jnp.exp2(s - new[:, :1]).astype(jnp.bfloat16)
            update = jnp.dot(w, value, preferred_element_type=jnp.float32)
            shrink = jnp.exp2(old - new)
            top[h] = new
            acc[h] = acc[h] * jnp.concatenate([shrink, shrink], axis=1) + update
        return carry

    lax.fori_loop(0, (active + 1) // 2, step, 0)

    packed = jnp.zeros((rows, 128), jnp.float32)
    for h in range(heads):
        total = jnp.maximum(acc[h, :, HEAD_SIZE:], 1e-30)
        out = acc[h, :, :HEAD_SIZE] / total
        o_ref[0, :, :, h * HEAD_SIZE : (h + 1) * HEAD_SIZE] = out.astype(jnp.bfloat16).reshape(
            2, tok, HEAD_SIZE
        )
        packed = jnp.where(lanes == h, top[h] + jnp.log2(total), packed)
    chosen, levels = 0.0, 0.0
    for k in range(2):
        level = packed[k * tok : (k + 1) * tok]
        l_ref[0, k] = jnp.transpose(level)[:8]
        hot = hot_ref[0, k]
        chosen = chosen + jnp.dot(hot, o_ref[0, k], preferred_element_type=jnp.float32)
        levels = levels + jnp.dot(
            hot.astype(jnp.float32),
            level,
            preferred_element_type=jnp.float32,
            precision=lax.Precision.HIGHEST,
        )
    co_ref[0] = chosen.astype(jnp.bfloat16)
    cl_ref[0] = levels


def flash(sizes, lengths, q, kv, hot):
    xs, _, tok, width = q.shape
    heads = width // HEAD_SIZE
    keys = kv.shape[0] * 4 * tok
    rows = 2 * tok
    picks = hot.shape[2]

    def whole(*shape):
        return pl.BlockSpec((1, *shape), lambda i: (i,) + (0,) * len(shape))

    return pl.pallas_call(
        functools.partial(flash_kernel, sizes, lengths.shape[0]),
        out_shape=(
            jax.ShapeDtypeStruct(q.shape, jnp.bfloat16),
            jax.ShapeDtypeStruct((xs, 2, 8, 128), jnp.float32),
            jax.ShapeDtypeStruct((xs, picks, width), jnp.bfloat16),
            jax.ShapeDtypeStruct((xs, picks, 128), jnp.float32),
        ),
        grid=(xs,),
        in_specs=[
            pl.BlockSpec(memory_space=pltpu.SMEM),
            whole(2, tok, width),
            pl.BlockSpec(memory_space=VMEM),
            whole(2, picks, 128),
        ],
        out_specs=(
            whole(2, tok, width),
            whole(2, 8, 128),
            whole(picks, width),
            whole(picks, 128),
        ),
        scratch_shapes=[
            VMEM((heads, rows, 2 * HEAD_SIZE), jnp.float32),
            VMEM((heads, rows, 128), jnp.float32),
            VMEM((rows, 128), jnp.int32),
            VMEM((rows, 128), jnp.int32),
            pltpu.SMEM((2 * sizes[1] + 2,), jnp.int32),
            pltpu.SMEM((2 * sizes[1] + 2,), jnp.int32),
        ],
        compiler_params=pltpu.CompilerParams(vmem_limit_bytes=32 << 20),
        cost_estimate=pl.CostEstimate(
            flops=4 * heads * xs * rows * keys * HEAD_SIZE // 3,
            bytes_accessed=4 << 20,
            transcendentals=heads * xs * rows * keys // 3,
        ),
        name="flash",
    )(lengths, q, kv, hot)


def shares_of(levels):
    highest = functools.reduce(jnp.maximum, levels)
    parts = [jnp.exp2(level - highest) for level in levels]
    total = functools.reduce(jnp.add, parts)
    return [part / total for part in parts]


def tail_kernel(
    sizes,
    width_full,
    o_ref,
    l_ref,
    co_ref,
    cl_ref,
    res_ref,
    gain_ref,
    ids_ref,
    ow_ref,
    lm_ref,
    att_ref,
    out_ref,
    obuf,
    lbuf,
    cobuf,
    clbuf,
    rbuf,
    wbuf,
    lmbuf,
    psend,
    pbuf,
    sqbuf,
    ubuf,
    g_ref,
    logits,
    arrived,
    kbuf,
    ybuf,
    xbuf,
    zbuf,
    w_sem,
    o_send,
    o_recv,
    l_send,
    l_recv,
    c_send,
    c_recv,
    r_send,
    r_recv,
    p_sem,
    s_send,
    s_recv,
    u_sem,
    y_sem,
    z_send,
    z_recv,
    x_send,
    x_recv,
    k_send,
    k_recv,
    e_send,
    e_recv,
    mk_sem,
    my_sem,
    mx_send,
    mx_recv,
    mz_send,
    mz_recv,
    mh_sem,
):
    xs, zs = sizes
    x, yh, z, kc = (lax.axis_index(n) for n in CTX)
    hd = lax.axis_index("head")
    oy, ok, oh = (lax.rem(yh + 1, 2), lax.rem(kc + 1, 2), lax.rem(hd + 1, 2))
    row_slot = 2 * yh + kc
    quarter = 2 * kc + yh
    half = width_full // 2
    wide = half // 4
    heads = o_ref.shape[3] // HEAD_SIZE
    z_order = sorted(range(1, zs), key=lambda d: min(d, zs - d))
    x_order = sorted(range(1, xs), key=lambda d: min(d, xs - d))
    near = ((0, 1), (1, 0), (1, 1))

    weights = []
    for j, side in enumerate((hd, oh)):
        col = pl.multiple_of(side * half + quarter * wide, 128)
        weights.append(
            pltpu.make_async_copy(ow_ref.at[:, pl.ds(col, wide)], wbuf.at[j], w_sem.at[j])
        )
        weights[-1].start()
    embedding = pltpu.make_async_copy(lm_ref, lmbuf, w_sem.at[2])
    embedding.start()

    peers = []
    for dx in range(xs):
        for dy in range(2):
            for dk in range(2):
                if dx or dy or dk:
                    peers.append(
                        {
                            "x": lax.rem(x + dx, xs),
                            "yh": lax.rem(yh + dy, 2),
                            "core": lax.rem(kc + dk, 2),
                        }
                    )
    for where in ({}, {"core": ok}, {"yh": oy}, {"yh": oy, "core": ok}):
        peers.append({"head": oh, **where})
    for dz in range(1, zs):
        peers.append({"z": lax.rem(z + dz, zs)})
    greet(peers)

    def c_copies(dx, dy, dk):
        where = {
            "x": lax.rem(x + dx, xs),
            "yh": lax.rem(yh + dy, 2),
            "core": lax.rem(kc + dk, 2),
        }
        at = where["x"]
        own = (x, yh, kc)
        return (
            remote(
                cl_ref.at[at],
                clbuf.at[own],
                c_send.at[0, 4 * dx + 2 * dy + dk],
                c_recv.at[0, 4 * x + row_slot],
                **where,
            ),
            remote(
                co_ref.at[at],
                cobuf.at[own],
                c_send.at[1, 4 * dx + 2 * dy + dk],
                c_recv.at[1, 4 * x + row_slot],
                **where,
            ),
        )

    c_order = [
        (dx, dy, dk)
        for dx in list(reversed(x_order)) + [0]
        for dy in (1, 0)
        for dk in (0, 1)
        if dx or dy or dk
    ]
    for each in c_order:
        for copy in c_copies(*each):
            copy.start()
    pltpu.make_async_copy(
        cl_ref.at[x], clbuf.at[x, yh, kc], c_recv.at[0, 4 * x + row_slot]
    ).start()
    pltpu.make_async_copy(
        co_ref.at[x], cobuf.at[x, yh, kc], c_recv.at[1, 4 * x + row_slot]
    ).start()

    def r_copy(dy, dk):
        ty, tk = (lax.rem(yh + dy, 2), lax.rem(kc + dk, 2))
        return remote(
            res_ref.at[2 * tk + ty],
            rbuf.at[row_slot],
            r_send.at[2 * dy + dk],
            r_recv.at[row_slot],
            yh=ty,
            core=tk,
        )

    for dy, dk in near:
        r_copy(dy, dk).start()
    pltpu.make_async_copy(res_ref.at[quarter], rbuf.at[row_slot], r_recv.at[row_slot]).start()

    def o_copies(dx, dk):
        tx, tk = (lax.rem(x + dx, xs), lax.rem(kc + dk, 2))
        where = {"x": tx, "core": tk}
        s, mine = (2 * dx + dk, 2 * x + kc)
        return (
            remote(l_ref.at[tx, tk], lbuf.at[x, kc], l_send.at[s], l_recv.at[mine], **where),
            remote(o_ref.at[tx, tk], obuf.at[x, kc], o_send.at[s], o_recv.at[mine], **where),
        )

    o_order = [
        (dx, dk) for dx in list(reversed(x_order)) + [0] for dk in (0, 1) if dx or dk
    ]
    for dx, dk in o_order:
        for copy in o_copies(dx, dk):
            copy.start()
    pltpu.make_async_copy(o_ref.at[x, kc], obuf.at[x, kc], o_recv.at[2 * x + kc]).start()
    pltpu.make_async_copy(l_ref.at[x, kc], lbuf.at[x, kc], l_recv.at[2 * x + kc]).start()

    for s in range(4 * xs):
        at = (s // 4, s // 2 % 2, s % 2)
        for i, buf in enumerate((clbuf, cobuf)):
            part = buf.at[at]
            remote(part, part, c_send.at[i, 0], c_recv.at[i, s], head=oh).wait_recv()
    pieces = []
    for k in range(2):
        shares = shares_of([clbuf[j, 0, k] + clbuf[j, 1, k] for j in range(xs)])
        values = [(cobuf[j, 0, k] + cobuf[j, 1, k]).astype(jnp.float32) for j in range(xs)]
        for h in range(heads):
            cols = slice(h * HEAD_SIZE, (h + 1) * HEAD_SIZE)
            merged = sum(shares[j][:, h : h + 1] * values[j][:, cols] for j in range(xs))
            pieces.append(merged.astype(jnp.bfloat16))
    chosen = jnp.concatenate(pieces, axis=1)

    for copy in weights:
        copy.wait()
    psend[...] = jnp.dot(chosen, wbuf[1], preferred_element_type=jnp.float32).astype(jnp.bfloat16)
    p_copy = remote(psend, pbuf, p_sem.at[0], p_sem.at[1], head=oh)
    p_copy.start()
    hidden = jnp.dot(chosen, wbuf[0], preferred_element_type=jnp.float32)
    for s in range(4):
        part = rbuf.at[s]
        remote(part, part, r_send.at[0], r_recv.at[s], head=oh).wait_recv()
    residual = (rbuf[0] + rbuf[1]) + (rbuf[2] + rbuf[3])
    p_copy.wait_recv()
    hidden = residual.astype(jnp.float32) + (hidden + pbuf[...].astype(jnp.float32))

    own = 4 * hd + row_slot
    sqbuf[own] = jnp.broadcast_to(jnp.sum(hidden * hidden, axis=1, keepdims=True), (16, 128))

    def s_copy(d):
        dh, dy, dk = (d // 4, d // 2 % 2, d % 2)
        return remote(
            sqbuf.at[own],
            sqbuf.at[own],
            s_send.at[d],
            s_recv.at[d],
            head=lax.rem(hd + dh, 2),
            yh=lax.rem(yh + dy, 2),
            core=lax.rem(kc + dk, 2),
        )

    for d in range(1, 8):
        s_copy(d).start()
    for d in range(1, 8):
        s_copy(d).wait_recv()
    squares = functools.reduce(jnp.add, [sqbuf[s] for s in range(8)])
    scale = lax.rsqrt(squares / width_full + 1e-05)[:, :1]
    ubuf[...] = (hidden * scale * gain_ref[quarter]).astype(jnp.bfloat16)

    mine = pl.ds(pl.multiple_of(quarter * wide, 128), wide)
    both = pl.ds(pl.multiple_of(kc * 2 * wide, 128), 2 * wide)
    here = pltpu.make_async_copy(ubuf, g_ref.at[x, z, :, mine], u_sem)
    here.start()
    y_copy = remote(ubuf, g_ref.at[x, z, :, mine], y_sem.at[0], y_sem.at[1], yh=oy)
    y_copy.start()
    here.wait()
    y_copy.wait_recv()

    def block(bx, bz):
        return g_ref.at[bx, bz, :, both]

    def z_copy(dz):
        to = lax.rem(z + dz, zs)
        return remote(block(x, z), block(x, z), z_send.at[dz], z_recv.at[dz], z=to)

    def x_copy(dx, dz):
        bz = lax.rem(z + zs - dz, zs)
        to = lax.rem(x + dx, xs)
        return remote(block(x, bz), block(x, bz), x_send.at[dx, dz], x_recv.at[dx, dz], x=to)

    def plane_of(dx):
        return lax.rem(x + xs - dx, xs)

    def k_copy(dx):
        plane = g_ref.at[plane_of(dx), :, :, both]
        return remote(plane, plane, k_send.at[dx], k_recv.at[dx], core=ok)

    def e_copy(dx):
        at = plane_of(dx)
        return remote(
            logits.at[at, oh], arrived.at[at], e_send.at[dx], e_recv.at[dx], head=oh
        )

    def project(dx):
        at = plane_of(dx)
        k_copy(dx).wait_recv()
        rows = g_ref[at].reshape(zs * 16, half)
        out = jnp.dot(rows, lmbuf[...], preferred_element_type=jnp.float32)
        logits[at] = out.astype(jnp.bfloat16).reshape(logits.shape[1:])
        e_copy(dx).start()

    def reduce_plane(dx):
        at = plane_of(dx)
        e_copy(dx).wait_recv()
        both_halves = logits[at, hd].astype(jnp.float32) + arrived[at].astype(jnp.float32)
        rows, width = both_halves.shape
        highest = jnp.max(both_halves, axis=1, keepdims=True)
        total = jnp.sum(jnp.exp(both_halves - highest), axis=1, keepdims=True)
        match = ids_ref[at] == lax.broadcasted_iota(jnp.int32, (rows, width), 1)
        target = jnp.sum(jnp.where(match, both_halves, 0.0), axis=1, keepdims=True)
        lane = lax.broadcasted_iota(jnp.int32, (rows, 128), 1)
        packed = jnp.where(lane == 0, highest, jnp.where(lane == 1, total, target))
        kbuf[kc, at] = jnp.transpose(packed)[:8]

    for dz in reversed(z_order):
        z_copy(dz).start()
    for dz in [0] + z_order:
        if dz:
            z_copy(dz).wait_recv()
        for dx in x_order:
            x_copy(dx, dz).start()
    k_copy(0).start()

    for s in range(2 * xs):
        at = (s // 2, s % 2)
        for buf, send, recv in ((lbuf, l_send, l_recv), (obuf, o_send, o_recv)):
            part = buf.at[at]
            remote(part, part, send.at[0], recv.at[s], head=oh).wait_recv()
    for k in range(2):
        parts = shares_of([lbuf[j, k] for j in range(xs)])
        parts.append(jnp.zeros((128 - 8 * xs, 128), jnp.float32))
        shares = jnp.transpose(jnp.concatenate(parts, axis=0))
        for h in range(heads):
            cols = slice(h * HEAD_SIZE, (h + 1) * HEAD_SIZE)
            merged = sum(
                shares[:, 8 * j + h : 8 * j + h + 1] * obuf[j, k, :, cols].astype(jnp.float32)
                for j in range(xs)
            )
            at = (k * heads + h) * HEAD_SIZE
            att_ref[:, at : at + HEAD_SIZE] = merged.astype(jnp.bfloat16)

    embedding.wait()
    project(0)
    last = 0
    for dx in x_order:
        for dz in [0] + z_order:
            x_copy(dx, dz).wait_recv()
        k_copy(dx).start()
        reduce_plane(last)
        project(dx)
        last = dx
    reduce_plane(last)

    def merge(buf, count):
        tops = [buf[i, :, 0:1] for i in range(count)]
        top = functools.reduce(jnp.maximum, tops)
        total = functools.reduce(
            jnp.add, [buf[i, :, 1:2] * jnp.exp(tops[i] - top) for i in range(count)]
        )
        target = functools.reduce(jnp.add, [buf[i, :, 2:3] for i in range(count)])
        return jnp.concatenate([top, total] + [target] * 6, axis=1)

    mk_copy = remote(kbuf.at[kc], kbuf.at[kc], mk_sem.at[0], mk_sem.at[1], core=ok)
    mk_copy.start()
    mk_copy.wait_recv()
    ybuf[yh] = merge(kbuf, 2)
    my_copy = remote(ybuf.at[yh], ybuf.at[yh], my_sem.at[0], my_sem.at[1], yh=oy)
    my_copy.start()
    my_copy.wait_recv()
    xbuf[x] = merge(ybuf, 2)

    def mx_copy(d):
        to = lax.rem(x + d, xs)
        return remote(xbuf.at[x], xbuf.at[x], mx_send.at[d], mx_recv.at[d], x=to)

    for d in range(1, xs):
        mx_copy(d).start()
    for d in range(1, xs):
        mx_copy(d).wait_recv()
    zbuf[z] = merge(xbuf, xs)

    def mz_copy(d):
        to = lax.rem(z + d, zs)
        return remote(zbuf.at[z], zbuf.at[z], mz_send.at[d], mz_recv.at[d], z=to)

    for d in range(1, zs):
        mz_copy(d).start()
    for d in range(1, zs):
        mz_copy(d).wait_recv()
    final = merge(zbuf, zs)
    final = final[:, 2:3] - final[:, 0:1] - jnp.log(final[:, 1:2])
    out_ref[hd] = jnp.broadcast_to(final, out_ref.shape[1:])
    mh_copy = remote(out_ref.at[hd], out_ref.at[hd], mh_sem.at[0], mh_sem.at[1], head=oh)
    mh_copy.start()
    mh_copy.wait_recv()

    for each in c_order:
        for copy in c_copies(*each):
            copy.wait_send()
    for dy, dk in near:
        r_copy(dy, dk).wait_send()
    for dx, dk in o_order:
        for copy in o_copies(dx, dk):
            copy.wait_send()
    p_copy.wait_send()
    for d in range(1, 8):
        s_copy(d).wait_send()
    y_copy.wait_send()
    for dz in z_order:
        z_copy(dz).wait_send()
    for dx in x_order:
        for dz in range(zs):
            x_copy(dx, dz).wait_send()
    for dx in range(xs):
        k_copy(dx).wait_send()
        e_copy(dx).wait_send()
    mk_copy.wait_send()
    my_copy.wait_send()
    for d in range(1, xs):
        mx_copy(d).wait_send()
    for d in range(1, zs):
        mz_copy(d).wait_send()
    mh_copy.wait_send()


def tail(sizes, o, l, co, cl, res, gain, ids, out_weight, lm_weight):
    xs, zs = sizes
    tok = o.shape[2]
    depth, width_full = out_weight.shape
    half, vocab = lm_weight.shape
    wide = half // 4
    side = zs * 8
    dma = pltpu.SemaphoreType.DMA
    bf16, f32 = (jnp.bfloat16, jnp.float32)
    hbm = pl.BlockSpec(memory_space=pltpu.HBM)
    return pl.pallas_call(
        functools.partial(tail_kernel, sizes, width_full),
        out_shape=(
            jax.ShapeDtypeStruct((tok, depth), bf16),
            jax.ShapeDtypeStruct((2, xs, 8, side), f32),
        ),
        in_specs=[pl.BlockSpec(memory_space=VMEM)] * 7 + [hbm] * 2,
        out_specs=(pl.BlockSpec(memory_space=VMEM),) * 2,
        scratch_shapes=[
            VMEM(o.shape, bf16),
            VMEM(l.shape, f32),
            VMEM((xs, 2, 2, *co.shape[1:]), bf16),
            VMEM((xs, 2, 2, *cl.shape[1:]), f32),
            VMEM((4, 16, wide), bf16),
            VMEM((2, depth, wide), bf16),
            VMEM((half, vocab), bf16),
            VMEM((16, wide), bf16),
            VMEM((16, wide), bf16),
            VMEM((8, 16, 128), f32),
            VMEM((16, wide), bf16),
            VMEM((xs, zs, 16, half), bf16),
            VMEM((xs, 2, side, vocab), bf16),
            VMEM((xs, side, vocab), bf16),
            VMEM((2, xs, 8, side), f32),
            VMEM((2, xs, 8, side), f32),
            VMEM((xs, xs, 8, side), f32),
            VMEM((zs, xs, 8, side), f32),
            dma((3,)),
            dma((2 * xs,)),
            dma((2 * xs,)),
            dma((2 * xs,)),
            dma((2 * xs,)),
            dma((2, 4 * xs)),
            dma((2, 4 * xs)),
            dma((4,)),
            dma((4,)),
            dma((2,)),
            dma((8,)),
            dma((8,)),
            dma,
            dma((2,)),
            dma((zs,)),
            dma((zs,)),
            dma((xs, zs)),
            dma((xs, zs)),
            dma((xs,)),
            dma((xs,)),
            dma((xs,)),
            dma((xs,)),
            dma((2,)),
            dma((2,)),
            dma((xs,)),
            dma((xs,)),
            dma((zs,)),
            dma((zs,)),
            dma((2,)),
        ],
        compiler_params=pltpu.CompilerParams(
            collective_id=1, has_side_effects=True, vmem_limit_bytes=48 << 20
        ),
        name="tail",
    )(o, l, co, cl, res, gain, ids, out_weight, lm_weight)


def per_device(
    sizes,
    queries,
    rotated_keys,
    value_matrix,
    doc_lengths,
    scored,
    residual,
    norm_gain,
    out_weight,
    lm_weight,
    token_ids,
    old_logp,
    advantage,
):
    xs, zs = sizes
    tok = queries.shape[0]
    x, yh, z, kc = (lax.axis_index(n) for n in CTX)
    hd = lax.axis_index("head")
    resp = scored.shape[0]
    half = residual.shape[1]
    mine = (jnp.arange(4, dtype=jnp.int32) == 2 * yh + kc)[:, None]
    spots = jnp.where(mine, scored[None, :], -1).reshape(4 * resp, 1)
    hot = (spots == jnp.arange(tok, dtype=jnp.int32)[None, :]).astype(jnp.bfloat16)
    kvs, qs, hots = exchange(sizes, rotated_keys, value_matrix, queries, hot)
    o, l, co, cl = flash(sizes, doc_lengths, qs, kvs, hots)

    res = jnp.where(mine[:, :, None], residual[None], 0).astype(jnp.bfloat16)
    res = jnp.transpose(res.reshape(4 * resp, 4, half // 4), (1, 0, 2))
    gain = norm_gain.reshape(4, 1, half // 4)
    vocab = lm_weight.shape[1]
    start = (((x * 2 + yh) * zs + z) * 2 + kc) * vocab
    ids = token_ids.reshape(xs, 2, 2, zs // 2, 2, resp).transpose(2, 0, 3, 1, 4, 5)
    ids = lax.dynamic_index_in_dim(ids.reshape(2, xs, -1, 1), hd, 0, keepdims=False) - start
    attended, found = tail(sizes, o, l, co, cl, res, gain, ids, out_weight, lm_weight)
    found = found[:, :, 0].reshape(2, xs, zs // 2, 2, 2, resp)
    log_probs = found.transpose(1, 3, 0, 2, 4, 5).reshape(-1)
    ratio = jnp.exp(jnp.clip(log_probs - old_logp, -4.0, 4.0))
    token_loss = -jnp.minimum(ratio * advantage, jnp.clip(ratio, 0.8, 1.2) * advantage)
    return (attended, log_probs, token_loss)


def solution(mesh, shape=(4, 2, 8, 2)):
    finer = Mesh(mesh.devices.reshape(*shape, mesh.shape["head"]), NAMES)
    placed = (
        P(CTX, "head"),
        P(CTX, "head"),
        P(CTX, "head"),
        P(),
        P(CTX),
        P(CTX, "head"),
        P("head"),
        P("head", None),
        P("head", CTX),
        P(),
        P(),
        P(),
    )
    return jax.shard_map(
        functools.partial(per_device, (shape[0], shape[2])),
        mesh=finer,
        in_specs=placed,
        out_specs=(P(CTX, "head"), P(), P()),
        check_vma=False,
    )
```

time: 163 us -> 157 us (0.963)
  Pallas kernels: 147 us -> 138 us
  local copies, waits for them, and re-layouts: 9.32 us -> 15.7 us
  matrix products: 2.33 us -> 0 us
  other arithmetic: 2.43 us -> 0.77 us
    pallas_call x3 -> x2, Pallas kernels: 107 us -> 98.3 us  [the longest x1 85.6 us: tail(): pl.pallas_call(functools.partial(tail_kernel, sizes, width_full), out_sha...]
    unnamed x22 -> x20, local copies, waits for them, and re-layouts: 7.25 us -> 12.6 us
    dot_general x1 -> x0, matrix products: 2.33 us -> none  [per_device(): jnp.dot(rows.reshape(count, half), lm_weight, preferred_element_type=jnp....]
where the time goes in v2:
time: 157 us; the launch traced here: 155 us
  Pallas kernels  138 us (88%)
  local copies, waits for them, and re-layouts  15.7 us (10%)
    pallas_call x1, Pallas kernels, tail(): pl.pallas_call(functools.partial(tail_kernel, sizes, width_full), out_sha...  85.6 us
    pallas_call x1, Pallas kernels, exchange(): pl.pallas_call(functools.partial(exchange_kernel, sizes), out_shape=(jax....  39.3 us
    pallas_call x1, Pallas kernels, flash(): pl.pallas_call(functools.partial(flash_kernel, sizes, lengths.shape[0]),...  12.7 us
    unnamed x20, local copies, waits for them, and re-layouts  12.6 us

profile of v2, /device:TPU:8, one launch (start us, length us, event | category | flops | bytes accessed | tf_op | source)
XLA Modules:
  0.0 154.9 jit_solution(14313080582530704254)
XLA Ops:
  0.7 0.1 broadcast_in_dim.50
  0.7 0.1 broadcast_in_dim.51
  0.8 0.7 broadcast_in_dim.52
  1.5 0.1 broadcast_in_dim.53
  1.6 0.1 fusion.1.hot_ref
  1.6 0.7 broadcast_in_dim.56
  2.4 0.1 fusion.res_ref
  2.5 0.8 reshape.60
  3.4 0.1 reshape.61
  3.5 0.1 copy.22.ids_ref
  3.7 0.9 copy-done.1
  4.6 0.8 copy-done.2
  5.5 0.8 copy-done.3
  6.3 39.3 %exchange.1 = (bf16[8,4,2,128,128]{4,3,2,1,0:T(8,128)(2,1)S(1)}, bf16[4,2,128,512]{3,2,1,0:T(8,128)(2,1)S(1)}, bf16[4,2,16,128]{3,2,1,0:T(8,128)(2,1)S(1)}) custom-call(bf16[128,256]{1,0:T(8,128)(2,1)S(1)} %copy-done.2, bf16[128,256]{1,0:T(8,128)(2,1)S(1)} %copy-done.3, bf16[128,1024]{1,0:T(8,128)(2,1)S(1)} %copy-done.1, bf16[16,128]{1,0:T(8,128)(2,1)S(1)} %fusion.1.hot_ref), custom_call_target="tpu_custom_call" | custom-call | tf_op jit(solution)/shard_map/exchange/pallas_call | solution.py:217
  45.7 0.6 copy-done.5
  46.3 12.7 %flash.1 = (bf16[4,2,128,512]{3,2,1,0:T(8,128)(2,1)S(1)}, f32[4,2,8,128]{3,2,1,0:T(8,128)S(1)}, bf16[4,16,512]{2,1,0:T(8,128)(2,1)S(1)}, f32[4,16,128]{2,1,0:T(8,128)S(1)}) custom-call(s32[8]{0:T(128)S(1)} %copy-done.5, bf16[4,2,128,512]{3,2,1,0:T(8,128)(2,1)S(1)} %get-tuple-element.12.q_ref, bf16[8,4,2,128,128]{4,3,2,1,0:T(8,128)(2,1)S(1)} %get-tuple-element.13.kv_ref, ...), custom_call_target="tpu_custom_call" | custom-call | flops 2863311616 | bytes 4194304 | tf_op jit(solution)/shard_map/flash/pallas_call | solution.py:364
  59.0 6.4 %copy.23.lm_ref = bf16[2048,1002]{1,0:T(8,128)(2,1)} copy(bf16[2048,1002]{0,1:T(8,128)(2,1)} %param.20) | data formatting | bytes 8208384 | tf_op args[8]
  65.4 2.2 %copy-done = bf16[2048,1002]{1,0:T(8,128)(2,1)S(1)} copy-done((bf16[2048,1002]{1,0:T(8,128)(2,1)S(1)}, bf16[2048,1002]{1,0:T(8,128)(2,1)}, u32[]{:S(2)}) %copy-start) | copy-done | bytes 4104216
  67.6 85.6 %tail.1 = (bf16[128,1024]{1,0:T(8,128)(2,1)S(1)}, f32[2,4,8,64]{3,2,1,0:T(8,128)S(1)}) custom-call(bf16[4,2,128,512]{3,2,1,0:T(8,128)(2,1)S(1)} %get-tuple-element.15.o_ref, f32[4,2,8,128]{3,2,1,0:T(8,128)S(1)} %get-tuple-element.16.l_ref, bf16[4,16,512]{2,1,0:T(8,128)(2,1)S(1)} %get-tuple-element.17.co_ref, f32[4,16,128]{2,1,0:T(8,128)S(1)} %get-tuple-element.18.cl_ref, ...), custom_call_target="tpu_custom_call" | custom-call | tf_op jit(solution)/shard_map/tail/pallas_call | solution.py:815
  153.2 0.1 reshape_squeeze.3
  153.4 0.1 reshape.62
  153.6 0.0 copy-start.6
  153.6 0.6 minimum_negate_fusion
  154.2 0.7 copy.31
  (19 shorter events, 0.2 us)
Async XLA Ops:
  3.7 1.0 copy-start.1
  4.6 0.8 copy-start.2
  5.5 0.8 copy-start.3
  45.6 0.7 copy-start.5
  59.0 6.4 %copy-start.4 = (f32[2048]{0:T(1024)S(1)}, f32[2048]{0:T(1024)}, u32[]{:S(2)}) copy-start(f32[2048]{0:T(1024)} %param.18) | copy-start | bytes 24580
  65.4 2.2 %copy-start = (bf16[2048,1002]{1,0:T(8,128)(2,1)S(1)}, bf16[2048,1002]{1,0:T(8,128)(2,1)}, u32[]{:S(2)}) copy-start(bf16[2048,1002]{1,0:T(8,128)(2,1)} %copy.23.lm_ref) | copy-start | bytes 12312580
  67.6 86.0 %copy-start.7 = (f32[512]{0:T(512)S(1)}, f32[512]{0:T(512)}, u32[]{:S(2)}) copy-start(f32[512]{0:T(512)} %param.23) | copy-start | bytes 6148
  67.6 86.0 %copy-start.8 = (f32[512]{0:T(512)S(1)}, f32[512]{0:T(512)}, u32[]{:S(2)}) copy-start(f32[512]{0:T(512)} %param.22) | copy-start | bytes 6148
  153.6 1.3 copy-start.6

commit v3 on v2

--- a/solution.py
+++ b/solution.py
@@ -42,9 +42,11 @@
     v_ref,
     q_ref,
     hot_ref,
+    res_ref,
     kvbuf,
     qbuf,
     hotbuf,
+    resbuf,
     first_send,
     first_recv,
     up_send,
@@ -55,6 +57,8 @@
     q_recv,
     h_send,
     h_recv,
+    r_send,
+    r_recv,
 ):
     xs, zs = sizes
     x, yh, z, kc = (lax.axis_index(n) for n in CTX)
@@ -143,6 +147,23 @@
         for copy in q_copies(dx, dk):
             copy.start()
 
+    near = ((0, 1), (1, 0), (1, 1))
+
+    def r_copy(dy, dk):
+        ty, tk = (lax.rem(yh + dy, 2), lax.rem(kc + dk, 2))
+        return remote(
+            res_ref.at[tk],
+            resbuf.at[mine],
+            r_send.at[2 * dy + dk],
+            r_recv.at[mine],
+            yh=ty,
+            core=tk,
+        )
+
+    for dy, dk in near:
+        r_copy(dy, dk).start()
+    pltpu.make_async_copy(res_ref.at[kc], resbuf.at[mine], r_recv.at[mine]).start()
+
     def first_wait(s):
         for i in range(2):
             part = kvbuf.at[z, s, i]
@@ -199,6 +220,11 @@
         for copy in first(0, 0):
             copy.wait_send()
 
+    for dy, dk in near:
+        r_copy(dy, dk).wait_send()
+    for s in range(4):
+        part = resbuf.at[s]
+        remote(part, part, r_send.at[0], r_recv.at[s], z=up).wait_recv()
     for dx, dk in q_order:
         for copy in q_copies(dx, dk):
             copy.wait_send()
@@ -209,7 +235,7 @@
         remote(part, part, h_send.at[0], h_recv.at[s], z=up).wait_recv()
 
 
-def exchange(sizes, k, v, q, hot):
+def exchange(sizes, k, v, q, hot, res):
     xs, zs = sizes
     tok = q.shape[0]
     full = (zs - 2) // 2
@@ -220,9 +246,10 @@
             jax.ShapeDtypeStruct((zs, 4, 2, tok, HEAD_SIZE), k.dtype),
             jax.ShapeDtypeStruct((xs, 2, tok, q.shape[1] // 2), q.dtype),
             jax.ShapeDtypeStruct((xs, 2, *hot.shape), hot.dtype),
+            jax.ShapeDtypeStruct((4, *res.shape[1:]), res.dtype),
         ),
-        in_specs=[pl.BlockSpec(memory_space=VMEM)] * 4,
-        out_specs=(pl.BlockSpec(memory_space=VMEM),) * 3,
+        in_specs=[pl.BlockSpec(memory_space=VMEM)] * 5,
+        out_specs=(pl.BlockSpec(memory_space=VMEM),) * 4,
         scratch_shapes=[
             dma((4, 2)),
             dma((4, 2)),
@@ -234,12 +261,14 @@
             dma((2 * xs,)),
             dma((2 * xs,)),
             dma((2 * xs,)),
+            dma((4,)),
+            dma((4,)),
         ],
         compiler_params=pltpu.CompilerParams(
             collective_id=0, has_side_effects=True, vmem_limit_bytes=24 << 20
         ),
         name="exchange",
-    )(k, v, q, hot)
+    )(k, v, q, hot, res)
 
 
 def flash_kernel(
@@ -425,7 +454,6 @@
     lbuf,
     cobuf,
     clbuf,
-    rbuf,
     wbuf,
     lmbuf,
     psend,
@@ -435,10 +463,8 @@
     g_ref,
     logits,
     arrived,
-    kbuf,
-    ybuf,
-    xbuf,
-    zbuf,
+    sbuf,
+    fbuf,
     w_sem,
     o_send,
     o_recv,
@@ -446,13 +472,10 @@
     l_recv,
     c_send,
     c_recv,
-    r_send,
-    r_recv,
     p_sem,
     s_send,
     s_recv,
     u_sem,
-    y_sem,
     z_send,
     z_recv,
     x_send,
@@ -461,30 +484,25 @@
     k_recv,
     e_send,
     e_recv,
-    mk_sem,
-    my_sem,
-    mx_send,
-    mx_recv,
-    mz_send,
-    mz_recv,
-    mh_sem,
+    m_send,
+    m_recv,
+    f_send,
+    f_recv,
 ):
     xs, zs = sizes
     x, yh, z, kc = (lax.axis_index(n) for n in CTX)
     hd = lax.axis_index("head")
-    oy, ok, oh = (lax.rem(yh + 1, 2), lax.rem(kc + 1, 2), lax.rem(hd + 1, 2))
+    ok, oh = (lax.rem(kc + 1, 2), lax.rem(hd + 1, 2))
     row_slot = 2 * yh + kc
-    quarter = 2 * kc + yh
     half = width_full // 2
-    wide = half // 4
+    wide = half // 2
     heads = o_ref.shape[3] // HEAD_SIZE
     z_order = sorted(range(1, zs), key=lambda d: min(d, zs - d))
     x_order = sorted(range(1, xs), key=lambda d: min(d, xs - d))
-    near = ((0, 1), (1, 0), (1, 1))
 
     weights = []
     for j, side in enumerate((hd, oh)):
-        col = pl.multiple_of(side * half + quarter * wide, 128)
+        col = pl.multiple_of(side * half + kc * wide, 128)
         weights.append(
             pltpu.make_async_copy(ow_ref.at[:, pl.ds(col, wide)], wbuf.at[j], w_sem.at[j])
         )
@@ -504,10 +522,11 @@
                             "core": lax.rem(kc + dk, 2),
                         }
                     )
-    for where in ({}, {"core": ok}, {"yh": oy}, {"yh": oy, "core": ok}):
+    for where in ({}, {"core": ok}):
         peers.append({"head": oh, **where})
     for dz in range(1, zs):
         peers.append({"z": lax.rem(z + dz, zs)})
+        peers.append({"z": lax.rem(z + dz, zs), "head": oh})
     greet(peers)
 
     def c_copies(dx, dy, dk):
@@ -552,21 +571,6 @@
         co_ref.at[x], cobuf.at[x, yh, kc], c_recv.at[1, 4 * x + row_slot]
     ).start()
 
-    def r_copy(dy, dk):
-        ty, tk = (lax.rem(yh + dy, 2), lax.rem(kc + dk, 2))
-        return remote(
-            res_ref.at[2 * tk + ty],
-            rbuf.at[row_slot],
-            r_send.at[2 * dy + dk],
-            r_recv.at[row_slot],
-            yh=ty,
-            core=tk,
-        )
-
-    for dy, dk in near:
-        r_copy(dy, dk).start()
-    pltpu.make_async_copy(res_ref.at[quarter], rbuf.at[row_slot], r_recv.at[row_slot]).start()
-
     def o_copies(dx, dk):
         tx, tk = (lax.rem(x + dx, xs), lax.rem(kc + dk, 2))
         where = {"x": tx, "core": tk}
@@ -592,8 +596,13 @@
             remote(part, part, c_send.at[i, 0], c_recv.at[i, s], head=oh).wait_recv()
     pieces = []
     for k in range(2):
-        shares = shares_of([clbuf[j, 0, k] + clbuf[j, 1, k] for j in range(xs)])
-        values = [(cobuf[j, 0, k] + cobuf[j, 1, k]).astype(jnp.float32) for j in range(xs)]
+        shares = shares_of(
+            [jnp.concatenate([clbuf[j, 0, k], clbuf[j, 1, k]], axis=0) for j in range(xs)]
+        )
+        values = [
+            jnp.concatenate([cobuf[j, yy, k].astype(jnp.float32) for yy in range(2)], axis=0)
+            for j in range(xs)
+        ]
         for h in range(heads):
             cols = slice(h * HEAD_SIZE, (h + 1) * HEAD_SIZE)
             merged = sum(shares[j][:, h : h + 1] * values[j][:, cols] for j in range(xs))
@@ -606,57 +615,51 @@
     p_copy = remote(psend, pbuf, p_sem.at[0], p_sem.at[1], head=oh)
     p_copy.start()
     hidden = jnp.dot(chosen, wbuf[0], preferred_element_type=jnp.float32)
-    for s in range(4):
-        part = rbuf.at[s]
-        remote(part, part, r_send.at[0], r_recv.at[s], head=oh).wait_recv()
-    residual = (rbuf[0] + rbuf[1]) + (rbuf[2] + rbuf[3])
+    residual = (res_ref[0] + res_ref[1]) + (res_ref[2] + res_ref[3])
     p_copy.wait_recv()
     hidden = residual.astype(jnp.float32) + (hidden + pbuf[...].astype(jnp.float32))
 
-    own = 4 * hd + row_slot
+    own = 2 * hd + kc
     sqbuf[own] = jnp.broadcast_to(jnp.sum(hidden * hidden, axis=1, keepdims=True), (16, 128))
 
     def s_copy(d):
-        dh, dy, dk = (d // 4, d // 2 % 2, d % 2)
         return remote(
             sqbuf.at[own],
             sqbuf.at[own],
             s_send.at[d],
             s_recv.at[d],
-            head=lax.rem(hd + dh, 2),
-            yh=lax.rem(yh + dy, 2),
-            core=lax.rem(kc + dk, 2),
-        )
-
-    for d in range(1, 8):
+            head=lax.rem(hd + d // 2, 2),
+            core=lax.rem(kc + d % 2, 2),
+        )
+
+    for d in range(1, 4):
         s_copy(d).start()
-    for d in range(1, 8):
+    for d in range(1, 4):
         s_copy(d).wait_recv()
-    squares = functools.reduce(jnp.add, [sqbuf[s] for s in range(8)])
+    squares = (sqbuf[0] + sqbuf[1]) + (sqbuf[2] + sqbuf[3])
     scale = lax.rsqrt(squares / width_full + 1e-05)[:, :1]
-    ubuf[...] = (hidden * scale * gain_ref[quarter]).astype(jnp.bfloat16)
-
-    mine = pl.ds(pl.multiple_of(quarter * wide, 128), wide)
-    both = pl.ds(pl.multiple_of(kc * 2 * wide, 128), 2 * wide)
-    here = pltpu.make_async_copy(ubuf, g_ref.at[x, z, :, mine], u_sem)
-    here.start()
-    y_copy = remote(ubuf, g_ref.at[x, z, :, mine], y_sem.at[0], y_sem.at[1], yh=oy)
-    y_copy.start()
-    here.wait()
-    y_copy.wait_recv()
+    ubuf[...] = (hidden * scale * gain_ref[kc]).astype(jnp.bfloat16)
+    both = pl.ds(pl.multiple_of(kc * wide, 128), wide)
 
     def block(bx, bz):
         return g_ref.at[bx, bz, :, both]
 
     def z_copy(dz):
         to = lax.rem(z + dz, zs)
-        return remote(block(x, z), block(x, z), z_send.at[dz], z_recv.at[dz], z=to)
+        return remote(ubuf, block(x, z), z_send.at[dz], z_recv.at[dz], z=to)
 
     def x_copy(dx, dz):
         bz = lax.rem(z + zs - dz, zs)
         to = lax.rem(x + dx, xs)
         return remote(block(x, bz), block(x, bz), x_send.at[dx, dz], x_recv.at[dx, dz], x=to)
 
+    def relay(dz):
+        bz = lax.rem(z + zs - dz, zs)
+        step = 1 if 2 * dz < zs - 2 else xs - 1
+        part = block(lax.rem(x + xs - step, xs), bz)
+        to = lax.rem(x + step, xs)
+        return remote(part, part, x_send.at[2, dz], x_recv.at[2, dz], x=to)
+
     def plane_of(dx):
         return lax.rem(x + xs - dx, xs)
 
@@ -674,11 +677,13 @@
         at = plane_of(dx)
         k_copy(dx).wait_recv()
         rows = g_ref[at].reshape(zs * 16, half)
-        out = jnp.dot(rows, lmbuf[...], preferred_element_type=jnp.float32)
+        out = lax.dot_general(
+            rows, lmbuf[...], (((1,), (1,)), ((), ())), preferred_element_type=jnp.float32
+        )
         logits[at] = out.astype(jnp.bfloat16).reshape(logits.shape[1:])
         e_copy(dx).start()
 
-    def reduce_plane(dx):
+    def reduce_plane(dx, packed):
         at = plane_of(dx)
         e_copy(dx).wait_recv()
         both_halves = logits[at, hd].astype(jnp.float32) + arrived[at].astype(jnp.float32)
@@ -688,17 +693,30 @@
         match = ids_ref[at] == lax.broadcasted_iota(jnp.int32, (rows, width), 1)
         target = jnp.sum(jnp.where(match, both_halves, 0.0), axis=1, keepdims=True)
         lane = lax.broadcasted_iota(jnp.int32, (rows, 128), 1)
-        packed = jnp.where(lane == 0, highest, jnp.where(lane == 1, total, target))
-        kbuf[kc, at] = jnp.transpose(packed)[:8]
+        for i, column in enumerate((highest, total, target)):
+            packed = jnp.where(lane == at + 8 * i, column, packed)
+        return packed
 
     for dz in reversed(z_order):
         z_copy(dz).start()
-    for dz in [0] + z_order:
+    here = pltpu.make_async_copy(ubuf, block(x, z), u_sem)
+    here.start()
+    here.wait()
+    z_seq = [0] + z_order
+    sides = [1, xs - 1] if xs > 2 else [1]
+    for dz in z_seq:
         if dz:
             z_copy(dz).wait_recv()
-        for dx in x_order:
+        for dx in sides:
             x_copy(dx, dz).start()
     k_copy(0).start()
+    for dz in z_seq:
+        for dx in sides:
+            x_copy(dx, dz).wait_recv()
+        if xs > 2:
+            relay(dz).start()
+    for dx in sides:
+        k_copy(dx).start()
 
     for s in range(2 * xs):
         at = (s // 2, s % 2)
@@ -719,95 +737,100 @@
             att_ref[:, at : at + HEAD_SIZE] = merged.astype(jnp.bfloat16)
 
     embedding.wait()
+    packed = jnp.zeros((zs * 8, 128), jnp.float32)
     project(0)
     last = 0
-    for dx in x_order:
-        for dz in [0] + z_order:
-            x_copy(dx, dz).wait_recv()
-        k_copy(dx).start()
-        reduce_plane(last)
+    for dx in sides:
         project(dx)
+        packed = reduce_plane(last, packed)
         last = dx
-    reduce_plane(last)
-
-    def merge(buf, count):
-        tops = [buf[i, :, 0:1] for i in range(count)]
+    if xs > 2:
+        for dz in z_seq:
+            relay(dz).wait_recv()
+        k_copy(2).start()
+        packed = reduce_plane(last, packed)
+        last = 2
+        project(2)
+    packed = reduce_plane(last, packed)
+    packed = jnp.transpose(packed)
+    mine = 4 * x + row_slot
+    for i in range(3):
+        sbuf[mine, i] = packed[8 * i : 8 * i + 8]
+
+    def merged(parts):
+        tops = [part[0] for part in parts]
         top = functools.reduce(jnp.maximum, tops)
         total = functools.reduce(
-            jnp.add, [buf[i, :, 1:2] * jnp.exp(tops[i] - top) for i in range(count)]
-        )
-        target = functools.reduce(jnp.add, [buf[i, :, 2:3] for i in range(count)])
-        return jnp.concatenate([top, total] + [target] * 6, axis=1)
-
-    mk_copy = remote(kbuf.at[kc], kbuf.at[kc], mk_sem.at[0], mk_sem.at[1], core=ok)
-    mk_copy.start()
-    mk_copy.wait_recv()
-    ybuf[yh] = merge(kbuf, 2)
-    my_copy = remote(ybuf.at[yh], ybuf.at[yh], my_sem.at[0], my_sem.at[1], yh=oy)
-    my_copy.start()
-    my_copy.wait_recv()
-    xbuf[x] = merge(ybuf, 2)
-
-    def mx_copy(d):
-        to = lax.rem(x + d, xs)
-        return remote(xbuf.at[x], xbuf.at[x], mx_send.at[d], mx_recv.at[d], x=to)
-
-    for d in range(1, xs):
-        mx_copy(d).start()
-    for d in range(1, xs):
-        mx_copy(d).wait_recv()
-    zbuf[z] = merge(xbuf, xs)
-
-    def mz_copy(d):
-        to = lax.rem(z + d, zs)
-        return remote(zbuf.at[z], zbuf.at[z], mz_send.at[d], mz_recv.at[d], z=to)
-
-    for d in range(1, zs):
-        mz_copy(d).start()
-    for d in range(1, zs):
-        mz_copy(d).wait_recv()
-    final = merge(zbuf, zs)
-    final = final[:, 2:3] - final[:, 0:1] - jnp.log(final[:, 1:2])
-    out_ref[hd] = jnp.broadcast_to(final, out_ref.shape[1:])
-    mh_copy = remote(out_ref.at[hd], out_ref.at[hd], mh_sem.at[0], mh_sem.at[1], head=oh)
-    mh_copy.start()
-    mh_copy.wait_recv()
+            jnp.add, [part[1] * jnp.exp(part[0] - top) for part in parts]
+        )
+        target = functools.reduce(jnp.add, [part[2] for part in parts])
+        return (top, total, target)
+
+    def m_copy(dx, dy, dk):
+        s = 4 * dx + 2 * dy + dk
+        return remote(
+            sbuf.at[mine],
+            sbuf.at[mine],
+            m_send.at[s],
+            m_recv.at[s],
+            x=lax.rem(x + dx, xs),
+            yh=lax.rem(yh + dy, 2),
+            core=lax.rem(kc + dk, 2),
+        )
+
+    for each in c_order:
+        m_copy(*each).start()
+    for each in c_order:
+        m_copy(*each).wait_recv()
+    for i, value in enumerate(merged([sbuf[s] for s in range(4 * xs)])):
+        fbuf[hd, z, i] = value
+
+    def f_copy(dh, dz):
+        part = fbuf.at[hd, z]
+        s = zs * dh + dz
+        where = {"head": lax.rem(hd + dh, 2), "z": lax.rem(z + dz, zs)}
+        return remote(part, part, f_send.at[s], f_recv.at[s], **where)
+
+    f_order = [(dh, dz) for dz in reversed([0] + z_order) for dh in (0, 1) if dh or dz]
+    for each in f_order:
+        f_copy(*each).start()
+    for each in f_order:
+        f_copy(*each).wait_recv()
+    for h in range(2):
+        top, total, target = merged([fbuf[h, zz] for zz in range(zs)])
+        out_ref[h] = target - top - jnp.log(total)
 
     for each in c_order:
         for copy in c_copies(*each):
             copy.wait_send()
-    for dy, dk in near:
-        r_copy(dy, dk).wait_send()
     for dx, dk in o_order:
         for copy in o_copies(dx, dk):
             copy.wait_send()
     p_copy.wait_send()
-    for d in range(1, 8):
+    for d in range(1, 4):
         s_copy(d).wait_send()
-    y_copy.wait_send()
     for dz in z_order:
         z_copy(dz).wait_send()
-    for dx in x_order:
-        for dz in range(zs):
+    for dz in range(zs):
+        for dx in sides:
             x_copy(dx, dz).wait_send()
+        if xs > 2:
+            relay(dz).wait_send()
     for dx in range(xs):
         k_copy(dx).wait_send()
         e_copy(dx).wait_send()
-    mk_copy.wait_send()
-    my_copy.wait_send()
-    for d in range(1, xs):
-        mx_copy(d).wait_send()
-    for d in range(1, zs):
-        mz_copy(d).wait_send()
-    mh_copy.wait_send()
+    for each in c_order:
+        m_copy(*each).wait_send()
+    for each in f_order:
+        f_copy(*each).wait_send()
 
 
 def tail(sizes, o, l, co, cl, res, gain, ids, out_weight, lm_weight):
     xs, zs = sizes
     tok = o.shape[2]
     depth, width_full = out_weight.shape
-    half, vocab = lm_weight.shape
-    wide = half // 4
+    vocab, half = lm_weight.shape
+    wide = half // 2
     side = zs * 8
     dma = pltpu.SemaphoreType.DMA
     bf16, f32 = (jnp.bfloat16, jnp.float32)
@@ -816,7 +839,7 @@
         functools.partial(tail_kernel, sizes, width_full),
         out_shape=(
             jax.ShapeDtypeStruct((tok, depth), bf16),
-            jax.ShapeDtypeStruct((2, xs, 8, side), f32),
+            jax.ShapeDtypeStruct((2, 8, side), f32),
         ),
         in_specs=[pl.BlockSpec(memory_space=VMEM)] * 7 + [hbm] * 2,
         out_specs=(pl.BlockSpec(memory_space=VMEM),) * 2,
@@ -825,20 +848,17 @@
             VMEM(l.shape, f32),
             VMEM((xs, 2, 2, *co.shape[1:]), bf16),
             VMEM((xs, 2, 2, *cl.shape[1:]), f32),
-            VMEM((4, 16, wide), bf16),
             VMEM((2, depth, wide), bf16),
-            VMEM((half, vocab), bf16),
+            VMEM((vocab, half), bf16),
             VMEM((16, wide), bf16),
             VMEM((16, wide), bf16),
-            VMEM((8, 16, 128), f32),
+            VMEM((4, 16, 128), f32),
             VMEM((16, wide), bf16),
             VMEM((xs, zs, 16, half), bf16),
             VMEM((xs, 2, side, vocab), bf16),
             VMEM((xs, side, vocab), bf16),
-            VMEM((2, xs, 8, side), f32),
-            VMEM((2, xs, 8, side), f32),
-            VMEM((xs, xs, 8, side), f32),
-            VMEM((zs, xs, 8, side), f32),
+            VMEM((4 * xs, 3, 8, side), f32),
+            VMEM((2, zs, 3, 8, side), f32),
             dma((3,)),
             dma((2 * xs,)),
             dma((2 * xs,)),
@@ -846,13 +866,10 @@
             dma((2 * xs,)),
             dma((2, 4 * xs)),
             dma((2, 4 * xs)),
+            dma((2,)),
             dma((4,)),
             dma((4,)),
-            dma((2,)),
-            dma((8,)),
-            dma((8,)),
             dma,
-            dma((2,)),
             dma((zs,)),
             dma((zs,)),
             dma((xs, zs)),
@@ -861,16 +878,13 @@
             dma((xs,)),
             dma((xs,)),
             dma((xs,)),
-            dma((2,)),
-            dma((2,)),
-            dma((xs,)),
-            dma((xs,)),
-            dma((zs,)),
-            dma((zs,)),
-            dma((2,)),
+            dma((4 * xs,)),
+            dma((4 * xs,)),
+            dma((2 * zs,)),
+            dma((2 * zs,)),
         ],
         compiler_params=pltpu.CompilerParams(
-            collective_id=1, has_side_effects=True, vmem_limit_bytes=48 << 20
+            collective_id=1, has_side_effects=True, vmem_limit_bytes=61 << 20
         ),
         name="tail",
     )(o, l, co, cl, res, gain, ids, out_weight, lm_weight)
@@ -898,20 +912,21 @@
     resp = scored.shape[0]
     half = residual.shape[1]
     mine = (jnp.arange(4, dtype=jnp.int32) == 2 * yh + kc)[:, None]
-    spots = jnp.where(mine, scored[None, :], -1).reshape(4 * resp, 1)
+    near = (jnp.arange(2, dtype=jnp.int32) == kc)[:, None]
+    spots = jnp.where(near, scored[None, :], -1).reshape(2 * resp, 1)
     hot = (spots == jnp.arange(tok, dtype=jnp.int32)[None, :]).astype(jnp.bfloat16)
-    kvs, qs, hots = exchange(sizes, rotated_keys, value_matrix, queries, hot)
+    res = jnp.where(mine[:, :, None], residual[None], 0).astype(jnp.bfloat16)
+    res = jnp.transpose(res.reshape(4 * resp, 2, half // 2), (1, 0, 2))
+    kvs, qs, hots, res = exchange(sizes, rotated_keys, value_matrix, queries, hot, res)
     o, l, co, cl = flash(sizes, doc_lengths, qs, kvs, hots)
 
-    res = jnp.where(mine[:, :, None], residual[None], 0).astype(jnp.bfloat16)
-    res = jnp.transpose(res.reshape(4 * resp, 4, half // 4), (1, 0, 2))
-    gain = norm_gain.reshape(4, 1, half // 4)
+    gain = norm_gain.reshape(2, 1, half // 2)
     vocab = lm_weight.shape[1]
     start = (((x * 2 + yh) * zs + z) * 2 + kc) * vocab
     ids = token_ids.reshape(xs, 2, 2, zs // 2, 2, resp).transpose(2, 0, 3, 1, 4, 5)
     ids = lax.dynamic_index_in_dim(ids.reshape(2, xs, -1, 1), hd, 0, keepdims=False) - start
-    attended, found = tail(sizes, o, l, co, cl, res, gain, ids, out_weight, lm_weight)
-    found = found[:, :, 0].reshape(2, xs, zs // 2, 2, 2, resp)
+    attended, found = tail(sizes, o, l, co, cl, res, gain, ids, out_weight, lm_weight.T)
+    found = found[:, :xs].reshape(2, xs, zs // 2, 2, 2, resp)
     log_probs = found.transpose(1, 3, 0, 2, 4, 5).reshape(-1)
     ratio = jnp.exp(jnp.clip(log_probs - old_logp, -4.0, 4.0))
     token_loss = -jnp.minimum(ratio * advantage, jnp.clip(ratio, 0.8, 1.2) * advantage)

time: 157 us -> 148 us (0.943)
  Pallas kernels: 138 us -> 133 us
  local copies, waits for them, and re-layouts: 15.7 us -> 11.5 us
    pallas_call x1, Pallas kernels: 85.6 us -> 80.5 us  [tail(): pl.pallas_call(functools.partial(tail_kernel, sizes, width_full), out_sha...]
    unnamed x20 -> x27, local copies, waits for them, and re-layouts: 12.6 us -> 8.41 us
where the time goes in v3:
time: 148 us; the launch traced here: 146 us
  Pallas kernels  133 us (90%)
  local copies, waits for them, and re-layouts  11.5 us (8%)
  other arithmetic  1.49 us (1%)
    pallas_call x1, Pallas kernels, tail(): pl.pallas_call(functools.partial(tail_kernel, sizes, width_full), out_sha...  80.5 us
    pallas_call x1, Pallas kernels, exchange(): pl.pallas_call(functools.partial(exchange_kernel, sizes), out_shape=(jax....  39.4 us
    pallas_call x1, Pallas kernels, flash(): pl.pallas_call(functools.partial(flash_kernel, sizes, lengths.shape[0]),...  12.7 us
    unnamed x27, local copies, waits for them, and re-layouts  8.41 us

profile of v3, /device:TPU:8, one launch (start us, length us, event | category | flops | bytes accessed | tf_op | source)
XLA Modules:
  0.0 146.4 jit_solution(16112312043587934109)
XLA Ops:
  0.7 0.1 broadcast_in_dim.54
  0.8 0.7 broadcast_in_dim.56
  1.7 0.7 broadcast_select_fusion
  2.4 0.1 select_n.21
  2.6 0.9 copy-done.1
  3.5 0.8 copy-done.3
  4.4 0.8 copy-done.4
  5.2 39.4 %exchange.1 = (bf16[8,4,2,128,128]{4,3,2,1,0:T(8,128)(2,1)S(1)}, bf16[4,2,128,512]{3,2,1,0:T(8,128)(2,1)S(1)}, bf16[4,2,8,128]{3,2,1,0:T(8,128)(2,1)S(1)}, bf16[4,16,1024]{2,1,0:T(8,128)(2,1)S(1)}) custom-call(bf16[128,256]{1,0:T(8,128)(2,1)S(1)} %copy-done.3, bf16[128,256]{1,0:T(8,128)(2,1)S(1)} %copy-done.4, bf16[128,1024]{1,0:T(8,128)(2,1)S(1)} %copy-done.1, ...), custom_call_target="tpu_custom_call" | custom-call | tf_op jit(solution)/shard_map/exchange/pallas_call | solution.py:243
  44.7 0.6 copy-done.2
  45.3 0.7 copy-done.8
  46.0 12.7 %flash.1 = (bf16[4,2,128,512]{3,2,1,0:T(8,128)(2,1)S(1)}, f32[4,2,8,128]{3,2,1,0:T(8,128)S(1)}, bf16[4,8,512]{2,1,0:T(8,128)(2,1)S(1)}, f32[4,8,128]{2,1,0:T(8,128)S(1)}) custom-call(s32[8]{0:T(128)S(1)} %copy-done.8, bf16[4,2,128,512]{3,2,1,0:T(8,128)(2,1)S(1)} %get-tuple-element.13.q_ref, bf16[8,4,2,128,128]{4,3,2,1,0:T(8,128)(2,1)S(1)} %get-tuple-element.14.kv_ref, ...), custom_call_target="tpu_custom_call" | custom-call | flops 2863311616 | bytes 4194304 | tf_op jit(solution)/shard_map/flash/pallas_call | solution.py:393
  58.7 1.0 copy-done
  59.7 0.6 copy-done.5
  60.3 0.6 copy-done.6
  60.9 0.6 copy-done.7
  61.5 0.1 reshape.65
  61.7 0.1 reshape.66
  61.8 0.8 copy.20.ids_ref
  62.6 80.5 %tail.1 = (bf16[128,1024]{1,0:T(8,128)(2,1)}, f32[2,8,64]{2,1,0:T(8,128)}) custom-call(bf16[4,2,128,512]{3,2,1,0:T(8,128)(2,1)} %copy-done, f32[4,2,8,128]{3,2,1,0:T(8,128)} %copy-done.5, bf16[4,8,512]{2,1,0:T(8,128)(2,1)} %copy-done.6, f32[4,8,128]{2,1,0:T(8,128)} %copy-done.7, bf16[4,16,1024]{2,1,0:T(8,128)(2,1)} %copy-done.2, f32[2,1,1024]{2,1,0:T(1,128)} %bitcast.13, ...), custom_call_target="tpu_custom_call" | custom-call | tf_op jit(solution)/shard_map/tail/pallas_call | solution.py:838
  143.1 0.7 slice.3
  143.8 0.1 reshape.67
  144.0 0.1 reshape.68
  144.2 0.6 minimum_negate_fusion
  144.8 1.7 %copy.28 = bf16[128,1024]{1,0:T(8,128)(2,1)} copy(bf16[128,1024]{1,0:T(8,128)(2,1)} %get-tuple-element.26) | data formatting | bytes 524288
  (26 shorter events, 0.4 us)
Async XLA Ops:
  2.6 0.9 copy-start.1
  3.5 0.8 copy-start.3
  4.4 0.8 copy-start.4
  44.6 0.7 copy-start.2
  45.3 0.7 copy-start.8
  46.0 15.5 %copy-start.10 = (s32[512]{0:T(512)S(1)}, s32[512]{0:T(512)}, u32[]{:S(2)}) copy-start(s32[512]{0:T(512)} %param.21) | copy-start | bytes 6148
  58.7 1.0 copy-start
  59.7 0.6 copy-start.5
  60.3 0.6 copy-start.6
  60.9 0.6 copy-start.7
  62.6 81.6 %copy-start.11 = (f32[512]{0:T(512)S(1)}, f32[512]{0:T(512)}, u32[]{:S(2)}) copy-start(f32[512]{0:T(512)} %param.23) | copy-start | bytes 6148
  62.6 81.6 %copy-start.12 = (f32[512]{0:T(512)S(1)}, f32[512]{0:T(512)}, u32[]{:S(2)}) copy-start(f32[512]{0:T(512)} %param.22) | copy-start | bytes 6148
  144.1 2.3 %copy-start.9 = (f32[512]{0:T(512)}, f32[512]{0:T(512)S(1)}, u32[]{:S(2)}) copy-start(f32[512]{0:T(512)S(1)} %reshape.68) | copy-start | bytes 6148

commit v4 on v3

--- a/solution.py
+++ b/solution.py
@@ -59,6 +59,7 @@
     h_recv,
     r_send,
     r_recv,
+    y_sem,
 ):
     xs, zs = sizes
     x, yh, z, kc = (lax.axis_index(n) for n in CTX)
@@ -86,16 +87,15 @@
     def columns(ref, head, width):
         return ref.at[:, pl.ds(pl.multiple_of(head * width, 128), width)]
 
-    def first(dy, dk):
-        ty, tk = (lax.rem(yh + dy, 2), lax.rem(kc + dk, 2))
+    def first(dk):
+        tk = lax.rem(kc + dk, 2)
         return [
             remote(
                 columns(ref, tk, HEAD_SIZE),
                 kvbuf.at[z, mine, i],
-                first_send.at[2 * dy + dk, i],
-                first_recv.at[mine, i],
+                first_send.at[dk, i],
+                first_recv.at[kc, i],
                 x=tx,
-                yh=ty,
                 core=tk,
             )
             for i, ref in enumerate((k_ref, v_ref))
@@ -104,14 +104,13 @@
     def first_here():
         return [
             pltpu.make_async_copy(
-                columns(ref, kc, HEAD_SIZE), kvbuf.at[z, mine, i], first_recv.at[mine, i]
+                columns(ref, kc, HEAD_SIZE), kvbuf.at[z, mine, i], first_recv.at[kc, i]
             )
             for i, ref in enumerate((k_ref, v_ref))
         ]
 
-    for dy, dk in ((1, 0), (1, 1), (0, 1)):
-        for copy in first(dy, dk):
-            copy.start()
+    for copy in first(1):
+        copy.start()
 
     @pl.when(shift == 0)
     def _():
@@ -120,7 +119,7 @@
 
     @pl.when(shift != 0)
     def _():
-        for copy in first(0, 0):
+        for copy in first(0):
             copy.start()
 
     def q_copies(dx, dk):
@@ -164,14 +163,22 @@
         r_copy(dy, dk).start()
     pltpu.make_async_copy(res_ref.at[kc], resbuf.at[mine], r_recv.at[mine]).start()
 
-    def first_wait(s):
+    def first_wait(k):
         for i in range(2):
-            part = kvbuf.at[z, s, i]
-            remote(part, part, first_send.at[0, i], first_recv.at[s, i], z=up).wait_recv()
+            part = kvbuf.at[z, 2 * yh + k, i]
+            remote(part, part, first_send.at[0, i], first_recv.at[k, i], z=up).wait_recv()
+
+    def across(side):
+        part = kvbuf.at[z, pl.ds(2 * side, 2)]
+        return remote(part, part, y_sem.at[0], y_sem.at[1], yh=lax.rem(yh + 1, 2))
+
+    for k in range(2):
+        first_wait(k)
+    across(yh).start()
 
     def ring(going_up, slot, t, h):
         send, recv, to = (up_send, up_recv, up) if going_up else (down_send, down_recv, down)
-        part = kvbuf.at[slot, pl.ds(2 * h, 2)]
+        part = kvbuf.at[slot, pl.ds(2 * lax.rem(yh + h, 2), 2)]
         return remote(part, part, send.at[t, h], recv.at[t, h], z=to)
 
     def sent(going_up, t, h):
@@ -185,16 +192,14 @@
     full = (zs - 2) // 2
     for t in range(full):
         for h in range(2):
-            if t == 0:
-                first_wait(2 * h)
-                first_wait(2 * h + 1)
+            if t == 0 and h == 1:
+                across(1 - yh).wait_recv()
             for going_up in (True, False):
                 if t > 0:
                     got(going_up, t - 1, h).wait_recv()
                 sent(going_up, t, h).start()
     if full == 0:
-        for s in range(4):
-            first_wait(s)
+        across(1 - yh).wait_recv()
     for going_up, h in ((True, 0), (False, 1)):
         if full > 0:
             got(going_up, full - 1, h).wait_recv()
@@ -211,13 +216,13 @@
                 sent(going_up, t, h).wait_send()
     sent(True, full, 0).wait_send()
     sent(False, full, 1).wait_send()
-    for dy, dk in ((1, 0), (1, 1), (0, 1)):
-        for copy in first(dy, dk):
-            copy.wait_send()
+    for copy in first(1):
+        copy.wait_send()
+    across(yh).wait_send()
 
     @pl.when(shift != 0)
     def _():
-        for copy in first(0, 0):
+        for copy in first(0):
             copy.wait_send()
 
     for dy, dk in near:
@@ -251,8 +256,8 @@
         in_specs=[pl.BlockSpec(memory_space=VMEM)] * 5,
         out_specs=(pl.BlockSpec(memory_space=VMEM),) * 4,
         scratch_shapes=[
-            dma((4, 2)),
-            dma((4, 2)),
+            dma((2, 2)),
+            dma((2, 2)),
             dma((full + 1, 2)),
             dma((full + 1, 2)),
             dma((full + 1, 2)),
@@ -263,6 +268,7 @@
             dma((2 * xs,)),
             dma((4,)),
             dma((4,)),
+            dma((2,)),
         ],
         compiler_params=pltpu.CompilerParams(
             collective_id=0, has_side_effects=True, vmem_limit_bytes=24 << 20
@@ -692,9 +698,13 @@
         total = jnp.sum(jnp.exp(both_halves - highest), axis=1, keepdims=True)
         match = ids_ref[at] == lax.broadcasted_iota(jnp.int32, (rows, width), 1)
         target = jnp.sum(jnp.where(match, both_halves, 0.0), axis=1, keepdims=True)
-        lane = lax.broadcasted_iota(jnp.int32, (rows, 128), 1)
+        lane = lax.broadcasted_iota(jnp.int32, packed.shape, 1)
+        row = lax.broadcasted_iota(jnp.int32, packed.shape, 0)
+        low = lax.rem(at, 2) * rows
+        here = (row >= low) & (row < low + rows)
         for i, column in enumerate((highest, total, target)):
-            packed = jnp.where(lane == at + 8 * i, column, packed)
+            column = jnp.concatenate([column, column], axis=0)
+            packed = jnp.where(here & (lane == at // 2 + 2 * i), column, packed)
         return packed
 
     for dz in reversed(z_order):
@@ -710,6 +720,8 @@
         for dx in sides:
             x_copy(dx, dz).start()
     k_copy(0).start()
+    embedding.wait()
+    project(0)
     for dz in z_seq:
         for dx in sides:
             x_copy(dx, dz).wait_recv()
@@ -717,6 +729,8 @@
             relay(dz).start()
     for dx in sides:
         k_copy(dx).start()
+    for dx in sides:
+        project(dx)
 
     for s in range(2 * xs):
         at = (s // 2, s % 2)
@@ -736,34 +750,28 @@
             at = (k * heads + h) * HEAD_SIZE
             att_ref[:, at : at + HEAD_SIZE] = merged.astype(jnp.bfloat16)
 
-    embedding.wait()
-    packed = jnp.zeros((zs * 8, 128), jnp.float32)
-    project(0)
-    last = 0
-    for dx in sides:
-        project(dx)
-        packed = reduce_plane(last, packed)
-        last = dx
+    packed = jnp.zeros((zs * 16, 128), jnp.float32)
+    packed = reduce_plane(0, packed)
     if xs > 2:
         for dz in z_seq:
             relay(dz).wait_recv()
         k_copy(2).start()
-        packed = reduce_plane(last, packed)
-        last = 2
+        packed = reduce_plane(1, packed)
         project(2)
-    packed = reduce_plane(last, packed)
-    packed = jnp.transpose(packed)
+        packed = reduce_plane(xs - 1, packed)
+        packed = reduce_plane(2, packed)
+    else:
+        packed = reduce_plane(1, packed)
     mine = 4 * x + row_slot
-    for i in range(3):
-        sbuf[mine, i] = packed[8 * i : 8 * i + 8]
+    sbuf[mine] = jnp.transpose(packed)[:8]
 
     def merged(parts):
-        tops = [part[0] for part in parts]
+        tops = [part[0:2] for part in parts]
         top = functools.reduce(jnp.maximum, tops)
         total = functools.reduce(
-            jnp.add, [part[1] * jnp.exp(part[0] - top) for part in parts]
-        )
-        target = functools.reduce(jnp.add, [part[2] for part in parts])
+            jnp.add, [part[2:4] * jnp.exp(part[0:2] - top) for part in parts]
+        )
+        target = functools.reduce(jnp.add, [part[4:6] for part in parts])
         return (top, total, target)
 
     def m_copy(dx, dy, dk):
@@ -782,8 +790,8 @@
         m_copy(*each).start()
     for each in c_order:
         m_copy(*each).wait_recv()
-    for i, value in enumerate(merged([sbuf[s] for s in range(4 * xs)])):
-        fbuf[hd, z, i] = value
+    top, total, target = merged([sbuf[s] for s in range(4 * xs)])
+    fbuf[hd, z] = jnp.concatenate([top, total, target, target], axis=0)
 
     def f_copy(dh, dz):
         part = fbuf.at[hd, z]
@@ -798,7 +806,8 @@
         f_copy(*each).wait_recv()
     for h in range(2):
         top, total, target = merged([fbuf[h, zz] for zz in range(zs)])
-        out_ref[h] = target - top - jnp.log(total)
+        found = target - top - jnp.log(total)
+        out_ref[h] = jnp.concatenate([found] * 4, axis=0)
 
     for each in c_order:
         for copy in c_copies(*each):
@@ -839,7 +848,7 @@
         functools.partial(tail_kernel, sizes, width_full),
         out_shape=(
             jax.ShapeDtypeStruct((tok, depth), bf16),
-            jax.ShapeDtypeStruct((2, 8, side), f32),
+            jax.ShapeDtypeStruct((2, 8, 2 * side), f32),
         ),
         in_specs=[pl.BlockSpec(memory_space=VMEM)] * 7 + [hbm] * 2,
         out_specs=(pl.BlockSpec(memory_space=VMEM),) * 2,
@@ -857,8 +866,8 @@
             VMEM((xs, zs, 16, half), bf16),
             VMEM((xs, 2, side, vocab), bf16),
             VMEM((xs, side, vocab), bf16),
-            VMEM((4 * xs, 3, 8, side), f32),
-            VMEM((2, zs, 3, 8, side), f32),
+            VMEM((4 * xs, 8, 2 * side), f32),
+            VMEM((2, zs, 8, 2 * side), f32),
             dma((3,)),
             dma((2 * xs,)),
             dma((2 * xs,)),
@@ -884,7 +893,7 @@
             dma((2 * zs,)),
         ],
         compiler_params=pltpu.CompilerParams(
-            collective_id=1, has_side_effects=True, vmem_limit_bytes=61 << 20
+            collective_id=1, has_side_effects=True, vmem_limit_bytes=50 << 20
         ),
         name="tail",
     )(o, l, co, cl, res, gain, ids, out_weight, lm_weight)
@@ -926,7 +935,7 @@
     ids = token_ids.reshape(xs, 2, 2, zs // 2, 2, resp).transpose(2, 0, 3, 1, 4, 5)
     ids = lax.dynamic_index_in_dim(ids.reshape(2, xs, -1, 1), hd, 0, keepdims=False) - start
     attended, found = tail(sizes, o, l, co, cl, res, gain, ids, out_weight, lm_weight.T)
-    found = found[:, :xs].reshape(2, xs, zs // 2, 2, 2, resp)
+    found = found[:, : xs // 2].reshape(2, xs, zs // 2, 2, 2, resp)
     log_probs = found.transpose(1, 3, 0, 2, 4, 5).reshape(-1)
     ratio = jnp.exp(jnp.clip(log_probs - old_logp, -4.0, 4.0))
     token_loss = -jnp.minimum(ratio * advantage, jnp.clip(ratio, 0.8, 1.2) * advantage)

time: 148 us -> 131 us (0.89)
  Pallas kernels: 133 us -> 122 us
  local copies, waits for them, and re-layouts: 11.5 us -> 5.78 us
    pallas_call x1, Pallas kernels: 80.5 us -> 66.8 us  [tail(): pl.pallas_call(functools.partial(tail_kernel, sizes, width_full), out_sha...]
    unnamed x27 -> x19, local copies, waits for them, and re-layouts: 8.41 us -> 4.01 us
    pallas_call x1, Pallas kernels: 12.7 us -> 16.9 us  [flash(): pl.pallas_call(functools.partial(flash_kernel, sizes, lengths.shape[0]),...]
    pallas_call x1, Pallas kernels: 39.4 us -> 37.9 us  [exchange(): pl.pallas_call(functools.partial(exchange_kernel, sizes), out_shape=(jax....]
where the time goes in v4:
time: 131 us; the launch traced here: 130 us
  Pallas kernels  122 us (93%)
  local copies, waits for them, and re-layouts  5.78 us (4%)
  other arithmetic  1.49 us (1%)
    pallas_call x1, Pallas kernels, tail(): pl.pallas_call(functools.partial(tail_kernel, sizes, width_full), out_sha...  66.8 us
    pallas_call x1, Pallas kernels, exchange(): pl.pallas_call(functools.partial(exchange_kernel, sizes), out_shape=(jax....  37.9 us
    pallas_call x1, Pallas kernels, flash(): pl.pallas_call(functools.partial(flash_kernel, sizes, lengths.shape[0]),...  16.9 us
    unnamed x19, local copies, waits for them, and re-layouts  4.01 us

profile of v4, /device:TPU:8, one launch (start us, length us, event | category | flops | bytes accessed | tf_op | source)
XLA Modules:
  0.0 129.6 jit_solution(4797673062249713406)
XLA Ops:
  0.7 0.1 broadcast_in_dim.53
  0.7 0.1 broadcast_in_dim.54
  0.8 0.7 broadcast_in_dim.56
  1.6 0.1 fusion.res_ref
  1.7 0.7 broadcast_select_fusion
  2.4 0.1 select_n.21
  2.5 0.1 fusion.1.hot_ref
  2.6 0.9 copy-done
  3.5 0.8 copy-done.1
  4.4 0.8 copy-done.2
  5.2 37.9 %exchange.1 = (bf16[8,4,2,128,128]{4,3,2,1,0:T(8,128)(2,1)S(1)}, bf16[4,2,128,512]{3,2,1,0:T(8,128)(2,1)S(1)}, bf16[4,2,8,128]{3,2,1,0:T(8,128)(2,1)S(1)}, bf16[4,16,1024]{2,1,0:T(8,128)(2,1)S(1)}) custom-call(bf16[128,256]{1,0:T(8,128)(2,1)S(1)} %copy-done.1, bf16[128,256]{1,0:T(8,128)(2,1)S(1)} %copy-done.2, bf16[128,1024]{1,0:T(8,128)(2,1)S(1)} %copy-done, ...), custom_call_target="tpu_custom_call" | custom-call | tf_op jit(solution)/shard_map/exchange/pallas_call | solution.py:248
  43.1 0.0 copy-start.4
  43.2 0.6 copy-done.4
  43.8 16.9 %flash.1 = (bf16[4,2,128,512]{3,2,1,0:T(8,128)(2,1)S(1)}, f32[4,2,8,128]{3,2,1,0:T(8,128)S(1)}, bf16[4,8,512]{2,1,0:T(8,128)(2,1)S(1)}, f32[4,8,128]{2,1,0:T(8,128)S(1)}) custom-call(s32[8]{0:T(128)S(1)} %copy-done.4, bf16[4,2,128,512]{3,2,1,0:T(8,128)(2,1)S(1)} %get-tuple-element.13.q_ref, bf16[8,4,2,128,128]{4,3,2,1,0:T(8,128)(2,1)S(1)} %get-tuple-element.14.kv_ref, ...), custom_call_target="tpu_custom_call" | custom-call | flops 2863311616 | bytes 4194304 | tf_op jit(solution)/shard_map/flash/pallas_call | solution.py:399
  60.7 0.2 reshape.65
  60.9 0.1 reshape.66
  61.0 0.1 copy.20.ids_ref
  61.2 0.0 copy-start.8
  61.2 66.8 %tail.1 = (bf16[128,1024]{1,0:T(8,128)(2,1)S(1)}, f32[2,8,128]{2,1,0:T(8,128)S(1)}) custom-call(bf16[4,2,128,512]{3,2,1,0:T(8,128)(2,1)S(1)} %get-tuple-element.16.o_ref, f32[4,2,8,128]{3,2,1,0:T(8,128)S(1)} %get-tuple-element.17.l_ref, bf16[4,8,512]{2,1,0:T(8,128)(2,1)S(1)} %get-tuple-element.18.co_ref, f32[4,8,128]{2,1,0:T(8,128)S(1)} %get-tuple-element.19.cl_ref, ...), custom_call_target="tpu_custom_call" | custom-call | tf_op jit(solution)/shard_map/tail/pallas_call | solution.py:847
  128.0 0.1 reshape.67
  128.2 0.1 reshape.68
  128.3 0.0 copy-start.5
  128.3 0.6 minimum_negate_fusion
  128.9 0.7 copy.28
  (18 shorter events, 0.1 us)
Async XLA Ops:
  2.6 0.9 copy-start
  3.5 0.8 copy-start.1
  4.4 0.8 copy-start.2
  43.1 0.7 copy-start.4
  43.8 16.9 %copy-start.6 = (s32[512]{0:T(512)S(1)}, s32[512]{0:T(512)}, u32[]{:S(2)}) copy-start(s32[512]{0:T(512)} %param.21) | copy-start | bytes 6148
  43.8 17.4 %copy-start.3 = (f32[2048]{0:T(1024)S(1)}, f32[2048]{0:T(1024)}, u32[]{:S(2)}) copy-start(f32[2048]{0:T(1024)} %param.18) | copy-start | bytes 24580
  61.2 67.1 %copy-start.7 = (f32[512]{0:T(512)S(1)}, f32[512]{0:T(512)}, u32[]{:S(2)}) copy-start(f32[512]{0:T(512)} %param.23) | copy-start | bytes 6148
  61.2 67.1 %copy-start.8 = (f32[512]{0:T(512)S(1)}, f32[512]{0:T(512)}, u32[]{:S(2)}) copy-start(f32[512]{0:T(512)} %param.22) | copy-start | bytes 6148
  128.3 1.3 %copy-start.5 = (f32[512]{0:T(512)}, f32[512]{0:T(512)S(1)}, u32[]{:S(2)}) copy-start(f32[512]{0:T(512)S(1)} %reshape.68) | copy-start | bytes 6148

commit v5 on v4

--- a/solution.py
+++ b/solution.py
@@ -41,12 +41,14 @@
     k_ref,
     v_ref,
     q_ref,
-    hot_ref,
-    res_ref,
+    scored_ref,
+    own_ref,
     kvbuf,
     qbuf,
     hotbuf,
     resbuf,
+    hot_ref,
+    res_ref,
     first_send,
     first_recv,
     up_send,
@@ -82,6 +84,21 @@
                     )
     peers.append({"z": up})
     peers.append({"z": down})
+    picks = scored_ref.shape[0]
+    row = lax.broadcasted_iota(jnp.int32, hot_ref.shape, 0)
+    lane = lax.broadcasted_iota(jnp.int32, hot_ref.shape, 1)
+    hot = jnp.zeros(hot_ref.shape, jnp.float32)
+    for i in range(picks):
+        hot = jnp.where((row == picks * kc + i) & (lane == scored_ref[i]), 1.0, hot)
+    hot_ref[...] = hot.astype(jnp.bfloat16)
+    wide = res_ref.shape[2]
+    row = lax.broadcasted_iota(jnp.int32, res_ref.shape[1:], 0)
+    for side in range(2):
+        own = own_ref[:, side * wide : (side + 1) * wide].astype(jnp.float32)
+        placed = jnp.zeros(res_ref.shape[1:], jnp.float32)
+        for i in range(picks):
+            placed = jnp.where(row == picks * mine + i, own[i : i + 1], placed)
+        res_ref[side] = placed.astype(jnp.bfloat16)
     greet(peers)
 
     def columns(ref, head, width):
@@ -240,9 +257,11 @@
         remote(part, part, h_send.at[0], h_recv.at[s], z=up).wait_recv()
 
 
-def exchange(sizes, k, v, q, hot, res):
+def exchange(sizes, k, v, q, scored, residual):
     xs, zs = sizes
     tok = q.shape[0]
+    picks, half = residual.shape
+    hot, res = ((2 * picks, tok), (4 * picks, half // 2))
     full = (zs - 2) // 2
     dma = pltpu.SemaphoreType.DMA
     return pl.pallas_call(
@@ -250,12 +269,20 @@
         out_shape=(
             jax.ShapeDtypeStruct((zs, 4, 2, tok, HEAD_SIZE), k.dtype),
             jax.ShapeDtypeStruct((xs, 2, tok, q.shape[1] // 2), q.dtype),
-            jax.ShapeDtypeStruct((xs, 2, *hot.shape), hot.dtype),
-            jax.ShapeDtypeStruct((4, *res.shape[1:]), res.dtype),
+            jax.ShapeDtypeStruct((xs, 2, *hot), jnp.bfloat16),
+            jax.ShapeDtypeStruct((4, *res), jnp.bfloat16),
         ),
-        in_specs=[pl.BlockSpec(memory_space=VMEM)] * 5,
+        in_specs=[
+            pl.BlockSpec(memory_space=VMEM),
+            pl.BlockSpec(memory_space=VMEM),
+            pl.BlockSpec(memory_space=VMEM),
+            pl.BlockSpec(memory_space=pltpu.SMEM),
+            pl.BlockSpec(memory_space=VMEM),
+        ],
         out_specs=(pl.BlockSpec(memory_space=VMEM),) * 4,
         scratch_shapes=[
+            VMEM(hot, jnp.bfloat16),
+            VMEM((2, *res), jnp.bfloat16),
             dma((2, 2)),
             dma((2, 2)),
             dma((full + 1, 2)),
@@ -274,7 +301,7 @@
             collective_id=0, has_side_effects=True, vmem_limit_bytes=24 << 20
         ),
         name="exchange",
-    )(k, v, q, hot, res)
+    )(k, v, q, scored, residual)
 
 
 def flash_kernel(
@@ -326,13 +353,10 @@
         where[active] = base
         active = active + jnp.where((base < first + rows) & (base + rows > low), 1, 0)
 
-    def step(pair, carry):
-        one = order[2 * pair]
-        whole = 2 * pair + 1 < active
-        two = jnp.where(whole, order[2 * pair + 1], one)
-        bases = (where[2 * pair], jnp.where(whole, where[2 * pair + 1], 1 << 28))
+    def attend(places):
         keys, values, biases = [], [], []
-        for chunk, base in zip((one, two), bases):
+        for place in places:
+            chunk, base = (order[place], where[place])
             zz, yy = (chunk // 2, lax.rem(chunk, 2))
             for k in range(2):
                 keys.append(kv_ref[zz, 2 * yy + k, 0])
@@ -358,9 +382,17 @@
             shrink = jnp.exp2(old - new)
             top[h] = new
             acc[h] = acc[h] * jnp.concatenate([shrink, shrink], axis=1) + update
+
+    def step(pair, carry):
+        attend((2 * pair, 2 * pair + 1))
         return carry
 
-    lax.fori_loop(0, (active + 1) // 2, step, 0)
+    lax.fori_loop(0, active // 2, step, 0)
+
+    @pl.when(lax.rem(active, 2) == 1)
+    def _():
+        attend((active - 1,))
+
 
     packed = jnp.zeros((rows, 128), jnp.float32)
     for h in range(heads):
@@ -722,16 +754,6 @@
     k_copy(0).start()
     embedding.wait()
     project(0)
-    for dz in z_seq:
-        for dx in sides:
-            x_copy(dx, dz).wait_recv()
-        if xs > 2:
-            relay(dz).start()
-    for dx in sides:
-        k_copy(dx).start()
-    for dx in sides:
-        project(dx)
-
     for s in range(2 * xs):
         at = (s // 2, s % 2)
         for buf, send, recv in ((lbuf, l_send, l_recv), (obuf, o_send, o_recv)):
@@ -749,6 +771,16 @@
             )
             at = (k * heads + h) * HEAD_SIZE
             att_ref[:, at : at + HEAD_SIZE] = merged.astype(jnp.bfloat16)
+
+    for dz in z_seq:
+        for dx in sides:
+            x_copy(dx, dz).wait_recv()
+        if xs > 2:
+            relay(dz).start()
+    for dx in sides:
+        k_copy(dx).start()
+    for dx in sides:
+        project(dx)
 
     packed = jnp.zeros((zs * 16, 128), jnp.float32)
     packed = reduce_plane(0, packed)
@@ -915,18 +947,13 @@
     advantage,
 ):
     xs, zs = sizes
-    tok = queries.shape[0]
     x, yh, z, kc = (lax.axis_index(n) for n in CTX)
     hd = lax.axis_index("head")
     resp = scored.shape[0]
     half = residual.shape[1]
-    mine = (jnp.arange(4, dtype=jnp.int32) == 2 * yh + kc)[:, None]
-    near = (jnp.arange(2, dtype=jnp.int32) == kc)[:, None]
-    spots = jnp.where(near, scored[None, :], -1).reshape(2 * resp, 1)
-    hot = (spots == jnp.arange(tok, dtype=jnp.int32)[None, :]).astype(jnp.bfloat16)
-    res = jnp.where(mine[:, :, None], residual[None], 0).astype(jnp.bfloat16)
-    res = jnp.transpose(res.reshape(4 * resp, 2, half // 2), (1, 0, 2))
-    kvs, qs, hots, res = exchange(sizes, rotated_keys, value_matrix, queries, hot, res)
+    kvs, qs, hots, res = exchange(
+        sizes, rotated_keys, value_matrix, queries, scored, residual
+    )
     o, l, co, cl = flash(sizes, doc_lengths, qs, kvs, hots)
 
     gain = norm_gain.reshape(2, 1, half // 2)

time: 131 us -> 130 us (level)
    pallas_call x1, Pallas kernels: 66.8 us -> 63.5 us  [tail(): pl.pallas_call(functools.partial(tail_kernel, sizes, width_full), out_sha...]
    pallas_call x1, Pallas kernels: 16.9 us -> 19.2 us  [flash(): pl.pallas_call(functools.partial(flash_kernel, sizes, lengths.shape[0]),...]
    unnamed x19 -> x23, local copies, waits for them, and re-layouts: 4.01 us -> 5.37 us
where the time goes in v5:
time: 130 us; the launch traced here: 129 us
  Pallas kernels  121 us (93%)
  local copies, waits for them, and re-layouts  6.11 us (5%)
    pallas_call x1, Pallas kernels, tail(): pl.pallas_call(functools.partial(tail_kernel, sizes, width_full), out_sha...  63.5 us
    pallas_call x1, Pallas kernels, exchange(): pl.pallas_call(functools.partial(exchange_kernel, sizes), out_shape=(jax....  38.6 us
    pallas_call x1, Pallas kernels, flash(): pl.pallas_call(functools.partial(flash_kernel, sizes, lengths.shape[0]),...  19.2 us
    unnamed x23, local copies, waits for them, and re-layouts  5.37 us

profile of v5, /device:TPU:8, one launch (start us, length us, event | category | flops | bytes accessed | tf_op | source)
XLA Modules:
  0.0 128.8 jit_solution(1782853223039962744)
XLA Ops:
  0.6 0.0 copy-start
  0.6 0.9 copy-done
  1.6 0.8 copy-done.1
  2.4 0.8 copy-done.2
  3.3 0.7 copy-done.3
  4.0 0.7 copy-done.5
  4.6 38.6 %exchange.1 = (bf16[8,4,2,128,128]{4,3,2,1,0:T(8,128)(2,1)S(1)}, bf16[4,2,128,512]{3,2,1,0:T(8,128)(2,1)S(1)}, bf16[4,2,8,128]{3,2,1,0:T(8,128)(2,1)S(1)}, bf16[4,16,1024]{2,1,0:T(8,128)(2,1)S(1)}) custom-call(bf16[128,256]{1,0:T(8,128)(2,1)S(1)} %copy-done.1, bf16[128,256]{1,0:T(8,128)(2,1)S(1)} %copy-done.2, bf16[128,1024]{1,0:T(8,128)(2,1)S(1)} %copy-done, ...), custom_call_target="tpu_custom_call" | custom-call | tf_op jit(solution)/shard_map/exchange/pallas_call | solution.py:267
  43.3 0.0 copy-start.6
  43.3 0.6 copy-done.6
  43.9 19.2 %flash.1 = (bf16[4,2,128,512]{3,2,1,0:T(8,128)(2,1)S(1)}, f32[4,2,8,128]{3,2,1,0:T(8,128)S(1)}, bf16[4,8,512]{2,1,0:T(8,128)(2,1)S(1)}, f32[4,8,128]{2,1,0:T(8,128)S(1)}) custom-call(s32[8]{0:T(128)S(1)} %copy-done.6, bf16[4,2,128,512]{3,2,1,0:T(8,128)(2,1)S(1)} %get-tuple-element.13.q_ref, bf16[8,4,2,128,128]{4,3,2,1,0:T(8,128)(2,1)S(1)} %get-tuple-element.14.kv_ref, ...), custom_call_target="tpu_custom_call" | custom-call | flops 2863311616 | bytes 4194304 | tf_op jit(solution)/shard_map/flash/pallas_call | solution.py:431
  63.2 0.0 copy-done.8
  63.2 0.2 reshape.36
  63.4 0.1 reshape.37
  63.5 0.1 copy.18.ids_ref
  63.6 0.0 copy-done.4
  63.6 0.0 copy-start.9
  63.7 0.0 copy-start.10
  63.7 63.5 %tail.1 = (bf16[128,1024]{1,0:T(8,128)(2,1)S(1)}, f32[2,8,128]{2,1,0:T(8,128)S(1)}) custom-call(bf16[4,2,128,512]{3,2,1,0:T(8,128)(2,1)S(1)} %get-tuple-element.16.o_ref, f32[4,2,8,128]{3,2,1,0:T(8,128)S(1)} %get-tuple-element.17.l_ref, bf16[4,8,512]{2,1,0:T(8,128)(2,1)S(1)} %get-tuple-element.18.co_ref, f32[4,8,128]{2,1,0:T(8,128)S(1)} %get-tuple-element.19.cl_ref, ...), custom_call_target="tpu_custom_call" | custom-call | tf_op jit(solution)/shard_map/tail/pallas_call | solution.py:879
  127.2 0.1 reshape.38
  127.4 0.1 reshape.39
  127.5 0.0 copy-start.7
  127.5 0.6 minimum_negate_fusion
  128.1 0.7 copy.23
  128.8 0.0 copy-done.7
  (12 shorter events, 0.1 us)
Async XLA Ops:
  0.6 1.0 copy-start
  1.6 0.8 copy-start.1
  2.4 0.8 copy-start.2
  3.3 0.7 copy-start.3
  4.0 0.7 copy-start.5
  43.3 0.7 copy-start.6
  43.9 19.2 %copy-start.8 = (s32[512]{0:T(512)S(1)}, s32[512]{0:T(512)}, u32[]{:S(2)}) copy-start(s32[512]{0:T(512)} %param.21) | copy-start | bytes 6148
  43.9 19.7 %copy-start.4 = (f32[2048]{0:T(1024)S(1)}, f32[2048]{0:T(1024)}, u32[]{:S(2)}) copy-start(f32[2048]{0:T(1024)} %param.18) | copy-start | bytes 24580
  63.6 63.9 %copy-start.9 = (f32[512]{0:T(512)S(1)}, f32[512]{0:T(512)}, u32[]{:S(2)}) copy-start(f32[512]{0:T(512)} %param.23) | copy-start | bytes 6148
  63.7 63.9 %copy-start.10 = (f32[512]{0:T(512)S(1)}, f32[512]{0:T(512)}, u32[]{:S(2)}) copy-start(f32[512]{0:T(512)} %param.22) | copy-start | bytes 6148
  127.5 1.3 %copy-start.7 = (f32[512]{0:T(512)}, f32[512]{0:T(512)S(1)}, u32[]{:S(2)}) copy-start(f32[512]{0:T(512)S(1)} %reshape.39) | copy-start | bytes 6148

commit v6 on v5

--- a/solution.py
+++ b/solution.py
@@ -693,7 +693,7 @@
 
     def relay(dz):
         bz = lax.rem(z + zs - dz, zs)
-        step = 1 if 2 * dz < zs - 2 else xs - 1
+        step = 1 if ([0] + z_order).index(dz) % 2 == 0 else xs - 1
         part = block(lax.rem(x + xs - step, xs), bz)
         to = lax.rem(x + step, xs)
         return remote(part, part, x_send.at[2, dz], x_recv.at[2, dz], x=to)

time: 130 us -> 129 us (level)
  no operation moved by 1% of the time
where the time goes in v6:
time: 129 us
  Pallas kernels  121 us (94%)
  local copies, waits for them, and re-layouts  6.11 us (5%)
    pallas_call x1, Pallas kernels, tail(): pl.pallas_call(functools.partial(tail_kernel, sizes, width_full), out_sha...  63.2 us
    pallas_call x1, Pallas kernels, exchange(): pl.pallas_call(functools.partial(exchange_kernel, sizes), out_shape=(jax....  38.6 us
    pallas_call x1, Pallas kernels, flash(): pl.pallas_call(functools.partial(flash_kernel, sizes, lengths.shape[0]),...  19.2 us
    unnamed x23, local copies, waits for them, and re-layouts  5.37 us

profile of v6, /device:TPU:8, one launch (start us, length us, event | category | flops | bytes accessed | tf_op | source)
XLA Modules:
  0.0 128.5 jit_solution(2400095810595272031)
XLA Ops:
  0.6 0.0 copy-start
  0.6 0.9 copy-done
  1.6 0.8 copy-done.1
  2.4 0.8 copy-done.2
  3.3 0.7 copy-done.3
  4.0 0.7 copy-done.5
  4.6 38.6 %exchange.1 = (bf16[8,4,2,128,128]{4,3,2,1,0:T(8,128)(2,1)S(1)}, bf16[4,2,128,512]{3,2,1,0:T(8,128)(2,1)S(1)}, bf16[4,2,8,128]{3,2,1,0:T(8,128)(2,1)S(1)}, bf16[4,16,1024]{2,1,0:T(8,128)(2,1)S(1)}) custom-call(bf16[128,256]{1,0:T(8,128)(2,1)S(1)} %copy-done.1, bf16[128,256]{1,0:T(8,128)(2,1)S(1)} %copy-done.2, bf16[128,1024]{1,0:T(8,128)(2,1)S(1)} %copy-done, ...), custom_call_target="tpu_custom_call" | custom-call | tf_op jit(solution)/shard_map/exchange/pallas_call | solution.py:267
  43.3 0.0 copy-start.6
  43.3 0.6 copy-done.6
  43.9 19.2 %flash.1 = (bf16[4,2,128,512]{3,2,1,0:T(8,128)(2,1)S(1)}, f32[4,2,8,128]{3,2,1,0:T(8,128)S(1)}, bf16[4,8,512]{2,1,0:T(8,128)(2,1)S(1)}, f32[4,8,128]{2,1,0:T(8,128)S(1)}) custom-call(s32[8]{0:T(128)S(1)} %copy-done.6, bf16[4,2,128,512]{3,2,1,0:T(8,128)(2,1)S(1)} %get-tuple-element.13.q_ref, bf16[8,4,2,128,128]{4,3,2,1,0:T(8,128)(2,1)S(1)} %get-tuple-element.14.kv_ref, ...), custom_call_target="tpu_custom_call" | custom-call | flops 2863311616 | bytes 4194304 | tf_op jit(solution)/shard_map/flash/pallas_call | solution.py:431
  63.2 0.0 copy-done.8
  63.2 0.2 reshape.36
  63.4 0.1 reshape.37
  63.5 0.1 copy.18.ids_ref
  63.6 0.0 copy-done.4
  63.6 0.0 copy-start.9
  63.7 0.0 copy-start.10
  63.7 63.2 %tail.1 = (bf16[128,1024]{1,0:T(8,128)(2,1)S(1)}, f32[2,8,128]{2,1,0:T(8,128)S(1)}) custom-call(bf16[4,2,128,512]{3,2,1,0:T(8,128)(2,1)S(1)} %get-tuple-element.16.o_ref, f32[4,2,8,128]{3,2,1,0:T(8,128)S(1)} %get-tuple-element.17.l_ref, bf16[4,8,512]{2,1,0:T(8,128)(2,1)S(1)} %get-tuple-element.18.co_ref, f32[4,8,128]{2,1,0:T(8,128)S(1)} %get-tuple-element.19.cl_ref, ...), custom_call_target="tpu_custom_call" | custom-call | tf_op jit(solution)/shard_map/tail/pallas_call | solution.py:879
  126.9 0.1 reshape.38
  127.1 0.1 reshape.39
  127.2 0.0 copy-done.10
  127.2 0.0 copy-start.7
  127.2 0.6 minimum_negate_fusion
  127.8 0.7 copy.23
  (12 shorter events, 0.1 us)
Async XLA Ops:
  0.6 1.0 copy-start
  1.6 0.8 copy-start.1
  2.4 0.8 copy-start.2
  3.3 0.7 copy-start.3
  4.0 0.7 copy-start.5
  43.3 0.7 copy-start.6
  43.9 19.2 %copy-start.8 = (s32[512]{0:T(512)S(1)}, s32[512]{0:T(512)}, u32[]{:S(2)}) copy-start(s32[512]{0:T(512)} %param.21) | copy-start | bytes 6148
  43.9 19.7 %copy-start.4 = (f32[2048]{0:T(1024)S(1)}, f32[2048]{0:T(1024)}, u32[]{:S(2)}) copy-start(f32[2048]{0:T(1024)} %param.18) | copy-start | bytes 24580
  63.6 63.6 %copy-start.9 = (f32[512]{0:T(512)S(1)}, f32[512]{0:T(512)}, u32[]{:S(2)}) copy-start(f32[512]{0:T(512)} %param.23) | copy-start | bytes 6148
  63.7 63.6 %copy-start.10 = (f32[512]{0:T(512)S(1)}, f32[512]{0:T(512)}, u32[]{:S(2)}) copy-start(f32[512]{0:T(512)} %param.22) | copy-start | bytes 6148
  127.2 1.3 %copy-start.7 = (f32[512]{0:T(512)}, f32[512]{0:T(512)S(1)}, u32[]{:S(2)}) copy-start(f32[512]{0:T(512)S(1)} %reshape.39) | copy-start | bytes 6148
